TPU v7x, 256 devices: a whole 4x4x8 slice. The times are simulated.
256 devices in a mesh: row: 16 (over y, x), col: 16 (over z, core).
Axes of the slice: x: 4, y: 4, z: 8, core: 2. Of those that a mesh axis runs over, the one named last changes fastest.
Arguments:
- trail: float32 [2, 16, 512, 2, 16, 512], P(None, 'row', None, None, 'col'), may hold values from -6 to 6
- panel: float32 [2, 16, 512, 512], P(None, 'row', None, 'col'), may hold values from -6 to 6
- row_basis: float32 [2, 16, 64, 512], P(None, 'row', None, 'col'), may hold values from -0.75 to 0.75
- row_coeff: float32 [2, 16, 64, 512], P(None, 'row', None, 'col'), may hold values from -0.25 to 0.25
- col_basis: float32 [2, 16, 64, 512], P(None, 'col', None, 'row'), may hold values from -0.75 to 0.75
- col_scaled: float32 [2, 16, 64, 512], P(None, 'col', None, 'row'), may hold values from -0.25 to 0.25
- pivot_basis: float32 [64, 512], P(None, 'col'), may hold values from -0.75 to 0.75
- pivot_scaled: float32 [64, 512], replicated, may hold values from -0.25 to 0.25
- sketch: float32 [64, 512], replicated, may hold values from -6 to 6
- perm: int32 [512], replicated, may hold values from 0 to 511, each once
- pair_kind: int32 [256], replicated, may hold values from 0 to 1
- pivot_values: float32 [3, 256], replicated, may hold values from -3 to 3, as said below
Outputs:
- trail_out: float32 [2, 16, 512, 2, 16, 512], P(None, 'row', None, None, 'col')
- basis_out: float32 [2, 16, 64, 512], P(None, 'row')
- coeff_out: float32 [2, 16, 64, 512], P(None, 'row')
Inputs may be any that keep to these rules, and one draw needn't show every extreme that they name: `pivot_values`: rows 0 and 1 have magnitudes between 0.5 and 0.7; row 2 has magnitude 1.2 or more.
All inputs are finite; a program needn't handle non-finite values.
Results may differ from a plain program's by a relative error of at most 0.00013.
Values sent between devices are 32-bit elements; how exact they have to be, the bound alone decides.
A program may use at most 64 MiB of HBM per device.

v0:
```python
import jax
import jax.numpy as jnp
from jax import lax
from jax.sharding import PartitionSpec as P


def gather_turned(arrays, axis, dims):
    turned = [jnp.moveaxis(a, dim, 0) for a, dim in zip(arrays, dims)]
    both = jnp.concatenate([t.reshape(len(t), -1) for t in turned], axis=1)
    filled, at, outs = (lax.all_gather(both, axis, axis=0, tiled=True), 0, [])
    for t, dim in zip(turned, dims):
        share = filled[:, at : at + t[0].size].reshape(-1, *t.shape[1:])
        outs.append(jnp.moveaxis(share, 0, dim))
        at += t[0].size
    return tuple(outs)


def total_of_pieces(array, axis):
    return lax.all_gather(array, axis).sum(0)


def pair_apply(rows, pair_kind, pivot_values):
    shaped = rows.reshape(rows.shape[:-1] + (rows.shape[-1] // 2, 2))
    first_in = shaped[..., 0]
    second_in = shaped[..., 1]
    diag_one = pivot_values[0]
    diag_two = pivot_values[1]
    offdiag = pivot_values[2]
    determinant = diag_one * diag_two - offdiag * offdiag
    twin = pair_kind == 1
    first = jnp.where(
        twin, (first_in * diag_two - second_in * offdiag) / determinant, first_in / diag_one
    )
    second = jnp.where(
        twin, (second_in * diag_one - first_in * offdiag) / determinant, second_in / diag_two
    )
    return jnp.stack([first, second], axis=-1).reshape(rows.shape)


def tri_solve(lower, rhs):
    return jax.vmap(lambda low, right: jax.scipy.linalg.solve_triangular(low, right, lower=True))(
        lower, rhs
    )


def body(
    trail,
    panel,
    row_basis,
    row_coeff,
    col_basis,
    col_scaled,
    pivot_basis,
    pivot_scaled,
    sketch,
    perm,
    pair_kind,
    pivot_values,
):
    highest = lax.Precision.HIGHEST
    width = sketch.shape[1]
    block = panel.shape[3]
    xrows, yrows = gather_turned((row_basis, row_coeff), "col", (3, 3))
    zcols, gcols = gather_turned((col_basis, col_scaled), "row", (3, 3))
    xrows = xrows[:, 0]
    yrows = yrows[:, 0]
    zcols = zcols[:, 0]
    gcols = gcols[:, 0]
    core = jnp.einsum("arp,bsp->arbs", yrows, gcols, precision=highest)
    left = jnp.einsum("arp,arbs->apbs", xrows, core, precision=highest)
    change = jnp.einsum("apbs,bsq->apbq", left, zcols, precision=highest)
    trail_out = trail - change[:, None, :, :, None, :]
    pcore = jnp.einsum("arp,sp->ars", yrows, pivot_scaled, precision=highest)
    pleft = jnp.einsum("arp,ars->aps", xrows, pcore, precision=highest)
    updated = panel[:, 0] - jnp.einsum("aps,sq->apq", pleft, pivot_basis, precision=highest)
    scaled_t = pair_apply(sketch, pair_kind, pivot_values)
    column_ids = lax.axis_index("col") * block + jnp.arange(block, dtype=jnp.int32)
    selector = (perm[:, None] == column_ids[None, :]).astype(jnp.float32)
    local_sketch = jnp.dot(scaled_t, selector, precision=highest)
    partial_range = jnp.einsum("apq,rq->arp", updated, local_sketch, precision=highest)
    range_t = total_of_pieces(partial_range, "col")
    gram = jnp.einsum("arp,asp->ars", range_t, range_t, precision=highest) / width
    basis = tri_solve(jnp.linalg.cholesky(gram), range_t)
    projected_part = jnp.einsum("arp,apq->arq", basis, updated, precision=highest)
    projected = lax.all_gather(projected_part, "col", axis=2, tiled=True)
    permuted = jnp.take(projected, perm, axis=2)
    coeff = pair_apply(permuted, pair_kind, pivot_values) / jnp.sqrt(jnp.float32(width))
    return (trail_out, basis[:, None], coeff[:, None])


def solution(mesh):
    return jax.shard_map(
        body,
        mesh=mesh,
        in_specs=(
            P(None, "row", None, None, "col", None),
            P(None, "row", None, "col"),
            P(None, "row", None, "col"),
            P(None, "row", None, "col"),
            P(None, "col", None, "row"),
            P(None, "col", None, "row"),
            P(None, "col"),
            P(),
            P(),
            P(),
            P(),
            P(),
        ),
        out_specs=(
            P(None, "row", None, None, "col", None),
            P(None, "row", None, None),
            P(None, "row", None, None),
        ),
        check_vma=False,
    )
```

profile of v0, /device:TPU:1, one launch (start us, length us, event | category | flops | bytes accessed | tf_op | source)
XLA Modules:
  0.0 150.3 jit_solution(10058551639044590301)
XLA Ops:
  7.2 0.0 copy-start
  7.2 0.0 all-gather.3.cloned.1.call-start
  7.3 0.8 broadcast_compare_fusion
  8.0 0.8 fusion.11
  8.8 0.8 copy.78
  9.6 0.1 reshape.159
  9.7 0.8 copy.79
  10.5 0.1 reshape.160
  10.6 1.0 copy.85
  11.6 22.7 %all_gather.16 = f32[512,256]{1,0:T(8,128)S(1)} all-gather(f32[32,256]{1,0:T(8,128)S(1)} %pad_maximum_fusion.2), channel_id=1, replica_groups=mesh['row'=16,'col'=16] {'col'}, dimensions={0}, use_global_device_ids=true | all-gather | bytes 557056 | tf_op jit(solution)/shard_map/all_gather | solution.py:10
  34.4 0.1 copy.81
  34.6 0.1 copy.80
  34.7 2.2 %broadcast_select_fusion.3 = (f32[64,256,1]{0,2,1:T(1,128)S(1)}, f32[64,256,1]{0,2,1:T(1,128)S(1)}) fusion(pred[256]{0:T(512)(128)(4,1)S(1)} %broadcast_compare_fusion, f32[64,256,2]{0,2,1:T(2,128)S(1)} %bitcast.108, f32[256]{0:T(256)S(1)} %bitcast.120, f32[256]{0:T(256)S(1)} %bitcast.126, f32[256]{0:T(256)S(1)} %bitcast.123, f32[256]{0:T(256)S(1)} %bitcast.117), kind=kLoop, calls=%fused_computation.11 | loop fusion | flops 196608 | bytes 266496 | tf_op jit(solution)/shard_map/jit(_where)/select_n | solution.py:31
  36.9 0.3 pad_maximum_fusion
  37.2 0.5 fusion.1
  37.7 0.4 fusion.14
  38.1 0.4 convolution_bitcast_fusion.1
  38.5 0.3 convolution_subtract_fusion
  38.8 1.1 convolution_bitcast_fusion
  40.0 0.0 all-gather.3.cloned.1.call-update
  40.0 0.2 broadcast_in_dim.45
  40.2 0.1 reshape.156
  40.3 0.1 reshape.157
  40.4 19.9 %all_gather.15 = f32[512,256]{1,0:T(8,128)S(1)} all-gather(f32[32,256]{1,0:T(8,128)S(1)} %pad_maximum_fusion.1), channel_id=1, replica_groups=mesh['row'=16,'col'=16] {'row'}, dimensions={0}, use_global_device_ids=true | all-gather | bytes 557056 | tf_op jit(solution)/shard_map/all_gather | solution.py:10
  60.3 0.1 copy.82
  60.5 0.1 copy.77
  60.6 11.0 %copy.84 = f32[2,1,512,2,1,512]{2,5,0,3,4,1:T(8,128)} copy(f32[2,1,512,2,1,512]{5,4,3,2,1,0:T(1,128)} %param.12) | data formatting | bytes 8388608 | tf_op args[0]
  71.6 0.5 fusion.12
  72.1 0.6 fusion.13
  72.7 6.7 %bitcast_subtract_fusion = f32[2,1,512,2,1,512]{2,5,0,3,4,1:T(8,128)} fusion(f32[2,1,512,2,1,512]{2,5,0,3,4,1:T(8,128)} %copy.84, f32[2,64,512,1]{2,1,3,0:T(8,128)S(1)} %bitcast.109, f32[2,512,2,64]{1,3,0,2:T(8,128)S(1)} %fusion.13), kind=kOutput, calls=%fused_computation.1 | convolution fusion | flops 806354944 | bytes 9175040 | tf_op jit(solution)/shard_map/apbs,bsq->apbq/dot_general | solution.py:71
  79.4 10.9 %copy.91 = f32[2,1,512,2,1,512]{5,4,3,2,1,0:T(1,128)} copy(f32[2,1,512,2,1,512]{2,5,0,3,4,1:T(8,128)} %bitcast_subtract_fusion) | data formatting | bytes 8388608
  90.3 0.0 all-gather.3.cloned.1.call-done
  90.3 2.6 %reduce_sum.9 = f32[2,64,512]{2,1,0:T(8,128)S(1)} reduce(f32[16,2,64,512]{3,2,1,0:T(8,128)} %bitcast.101, f32[]{:T(128)} %constant.67.clone.1), dimensions={0}, to_apply=%region_0.1 | reduce | flops 983040 | bytes 4456452 | tf_op jit(solution)/shard_map/reduce_sum | solution.py:19
  93.0 0.4 fusion.15
  93.4 0.1 copy.87
  93.5 11.7 %custom-call.8 = f32[2,64,64]{2,1,0:T(8,128)S(1)} custom-call(f32[2,64,64]{2,1,0:T(8,128)S(1)} %fusion.7), custom_call_target="Cholesky" | custom-call | tf_op jit(solution)/shard_map/jit(cholesky)/cholesky | solution.py:83
  105.2 0.1 compare_reduce_fusion
  105.3 0.1 select_bitcast_fusion
  105.4 9.8 %custom-call.9 = f32[2,1,64,64]{2,3,1,0:T(8,128)S(1)} custom-call(f32[2,1,64,64]{3,2,1,0:T(8,128)S(1)} %select_bitcast_fusion), custom_call_target="InvertDiagBlocksLowerTriangular" | custom-call | tf_op jit(solution)/shard_map/vmap(jit(_solve_triangular))/triangular_solve | solution.py:41
  115.3 0.4 fusion.5
  115.7 0.3 fusion.16
  116.1 20.6 %all_gather.19 = f32[2,64,512]{1,2,0:T(8,128)S(1)} all-gather(f32[2,64,32]{1,2,0:T(8,128)S(1)} %fusion.16), channel_id=1, replica_groups=mesh['row'=16,'col'=16] {'col'}, dimensions={2}, use_global_device_ids=true | all-gather | bytes 278528 | tf_op jit(solution)/shard_map/all_gather | solution.py:85
  136.6 0.4 copy.89
  137.0 2.1 %gather_fusion = f32[512,2,64]{2,1,0:T(2,128)S(1)} fusion(f32[2,64,512]{1,0,2:T(2,128)S(1)} %copy.89, s32[1024]{0:T(1024)S(1)} %pad_clamp_fusion), kind=kCustom, calls=%fused_computation | custom fusion | bytes 526336 | tf_op jit(solution)/shard_map/jit(_take)/gather | solution.py:86
  139.1 0.6 copy_select_fusion
  139.8 2.2 %broadcast_select_fusion.1 = (f32[2,64,256,1]{1,3,2,0:T(1,128)S(1)}, f32[2,64,256,1]{1,3,2,0:T(1,128)S(1)}) fusion(pred[256]{0:T(512)(128)(4,1)S(1)} %broadcast_compare_fusion, f32[2,64,256,2]{1,3,2,0:T(2,128)S(1)} %copy_select_fusion, f32[256]{0:T(256)S(1)} %bitcast.122, f32[256]{0:T(256)S(1)} %multiply_subtract_fusion, f32[256]{0:T(256)S(1)} %bitcast.125, ...), kind=kLoop, calls=%fused_computation.8 | loop fusion | flops 393216 | bytes 528640 | tf_op jit(solution)/shard_map/jit(_where)/select_n | solution.py:31
  142.0 0.6 maximum_multiply_fusion
  142.6 0.9 copy.93
  (28 shorter events, 0.3 us)
Async XLA Ops:
  7.2 30.0 %copy-start = (f32[64,512]{1,0:T(8,128)S(1)}, f32[64,512]{1,0:T(8,128)}, u32[]{:S(2)}) copy-start(f32[64,512]{1,0:T(8,128)} %param.19) | copy-start | bytes 393220
  7.2 30.9 %copy-start.5 = (s32[512]{0:T(512)S(1)}, s32[512]{0:T(512)}, u32[]{:S(2)}) copy-start(s32[512]{0:T(512)} %param.21) | copy-start | bytes 6148
  7.2 31.3 %copy-start.6 = (f32[64,32]{0,1:T(8,128)S(1)}, f32[64,32]{0,1:T(8,128)}, u32[]{:S(2)}) copy-start(f32[64,32]{0,1:T(8,128)} %param.18) | copy-start | bytes 24580
  7.2 31.3 %copy-start.2 = (f32[2,1,512,32]{2,3,1,0:T(8,128)S(1)}, f32[2,1,512,32]{2,3,1,0:T(8,128)}, u32[]{:S(2)}) copy-start(f32[2,1,512,32]{2,3,1,0:T(8,128)} %param.13) | copy-start | bytes 393220
  7.2 33.0 %copy-start.3 = (f32[2,1,64,32]{2,3,1,0:T(8,128)S(1)}, f32[2,1,64,32]{2,3,1,0:T(8,128)}, u32[]{:S(2)}) copy-start(f32[2,1,64,32]{2,3,1,0:T(8,128)} %param.16) | copy-start | bytes 49156
  7.2 33.1 %copy-start.4 = (f32[2,1,64,32]{2,3,1,0:T(8,128)S(1)}, f32[2,1,64,32]{2,3,1,0:T(8,128)}, u32[]{:S(2)}) copy-start(f32[2,1,64,32]{2,3,1,0:T(8,128)} %param.17) | copy-start | bytes 49156
  7.2 83.1 %all-gather.3.cloned.1.call-start = ((), (), s32[]{:S(2)}) async-start(), calls=%async_computation | async-start | bytes 4456448 | tf_op jit(solution)/shard_map/all_gather | solution.py:19
  115.7 27.8 %copy-start.1 = (f32[2,64,512]{2,1,0:T(8,128)}, f32[2,64,512]{2,1,0:T(8,128)S(1)}, u32[]{:S(2)}) copy-start(f32[2,64,512]{2,1,0:T(8,128)S(1)} %fusion.5) | copy-start | bytes 786436
Sparse Core Ops, SparseCore 0:
  40.1 40.0 all-gather.2
where the time goes:
time: 151 us; the launch traced here: 150 us
  blocking collectives  63.2 us (42%)
  other arithmetic  32 us (21%)
  local copies, waits for them, and re-layouts  29.1 us (19%)
  between operations  14.4 us (10%)
  matrix products  11.7 us (8%)
    all_gather x2, blocking collectives, gather_turned(): filled, at, outs = (lax.all_gather(both, axis, axis=0, tiled=True), 0, [])  42.6 us
    unnamed x18, local copies, waits for them, and re-layouts  23.8 us
    all_gather x1, blocking collectives, body(): projected = lax.all_gather(projected_part, 'col', axis=2, tiled=True)  20.6 us
    another operation x4, other arithmetic, body(): basis = tri_solve(jnp.linalg.cholesky(gram), range_t)  11.9 us
    another operation x3, other arithmetic, tri_solve(): jax.scipy.linalg.solve_triangular(low, right, lower=True)  9.92 us
    dot_general x1, matrix products, body(): change = jnp.einsum('apbs,bsq->apbq', left, zcols, precision=highest)  6.7 us
    select_n x2, other arithmetic, pair_apply(): jnp.where(twin, (first_in * diag_two - second_in * offdiag) / determinant...  4.37 us
  transfers between devices with their start and end apart: 1, of which 0 were waited for; matrix products, arithmetic and copies ran while one was open for 20% of the time, Pallas kernels for 0%

commit v1 on v0

v1 whole, which is shorter than its diff:
```python
import functools

import jax
import jax.numpy as jnp
from jax import lax
from jax.experimental import pallas as pl
from jax.experimental.pallas import tpu as pltpu
from jax.sharding import PartitionSpec as P

MESH = pl.DeviceIdType.MESH
F32 = jnp.float32
BF16 = jnp.bfloat16
HIGHEST = lax.Precision.HIGHEST
NN = (((1,), (0,)), ((), ()))
NT = (((1,), (1,)), ((), ()))
TN = (((0,), (0,)), ((), ()))
VMEM = pl.BlockSpec(memory_space=pltpu.VMEM)


def dot(a, b, dims=NN):
    return lax.dot_general(a, b, dims, precision=HIGHEST, preferred_element_type=F32)


def split3(x):
    high = x.astype(BF16)
    rest = x - high.astype(F32)
    mid = rest.astype(BF16)
    low = (rest - mid.astype(F32)).astype(BF16)
    return jnp.concatenate([high, mid, low], axis=0)


def select_dot(x, chosen, dims):
    n = x.shape[0]
    out = lax.dot_general(split3(x), chosen, dims, preferred_element_type=F32)
    return (out[2 * n :] + out[n : 2 * n]) + out[:n]


def lower_half(shape):
    return lax.broadcasted_iota(jnp.int32, shape, 1) % 128 < 64


def swap(x):
    return pltpu.roll(x, 64, 1)


def fold(x):
    return jnp.where(lower_half((32, 128)), x[:32], swap(x[32:]))


def unfold(ref):
    low = lower_half((32, 128))
    tops, bottoms = [], []
    for j in range(4):
        even, odd = ref[2 * j], ref[2 * j + 1]
        tops.append(jnp.where(low, even, swap(odd)))
        bottoms.append(jnp.where(low, swap(even), odd))
    return jnp.concatenate([jnp.concatenate(tops, axis=1), jnp.concatenate(bottoms, axis=1)], axis=0)


def inverse_factor(gram):
    rows = lax.broadcasted_iota(jnp.int32, (64, 64), 0)
    eye = (rows == lax.broadcasted_iota(jnp.int32, (64, 64), 1)).astype(F32)
    both = jnp.concatenate([gram, eye], axis=1)
    work = [both[8 * g : 8 * g + 8] for g in range(8)]
    sub = lax.broadcasted_iota(jnp.int32, (8, 128), 0)
    for k in range(8):
        columns = {
            (g, j): jnp.broadcast_to(work[g][:, 8 * k + j : 8 * k + j + 1], (8, 128))
            for g in range(k, 8)
            for j in range(8)
        }
        pivots = jnp.ones((8, 128), F32)
        for j in range(8):
            pivot = jnp.broadcast_to(columns[k, j][j : j + 1], (8, 128))
            pivots = jnp.where(sub == j, pivot, pivots)
            inverse = 1.0 / pivot
            scaled = jnp.broadcast_to(work[k][j : j + 1], (8, 128)) * inverse
            heads = {
                later: jnp.broadcast_to(columns[k, later][j : j + 1], (8, 128)) * inverse
                for later in range(j + 1, 8)
            }
            for g in range(k, 8):
                factor = columns[g, j]
                if g == k:
                    if j == 7:
                        continue
                    factor = jnp.where(sub > j, factor, 0.0)
                work[g] = work[g] - factor * scaled
                for later in range(j + 1, 8):
                    columns[g, later] = columns[g, later] - factor * heads[later]
        work[k] = work[k] * lax.rsqrt(pivots)
    return jnp.concatenate(work, axis=0)


def panel_kernel(
    n_row,
    panel,
    row_basis,
    row_coeff,
    col_basis,
    col_scaled,
    pivot_basis,
    pivot_scaled,
    sketch,
    perm,
    pair_kind,
    pivot_values,
    xy,
    zg,
    ranges,
    coeffs,
    inverses,
    pan_send,
    pan_recv,
    pan_chip,
    pan_full,
    xy_send,
    zg_send,
    rng_send,
    rng_recv,
    c_send,
    c_recv,
    basis_full,
    chosen,
    updated,
    pan_ss,
    pan_rs,
    xy_ss,
    xy_rs,
    zg_ss,
    zg_rs,
    rng_ss,
    rng_rs,
    c_ss,
    c_rs,
    peer_ss,
    peer_rs,
):
    r = lax.axis_index("row")
    c = lax.axis_index("col")
    z = c // 2
    k = c % 2
    peer = 2 * z + 1 - k

    barrier = pltpu.get_barrier_semaphore()
    for d in range(1, 16):
        pl.semaphore_signal(barrier, inc=1, device_id=(r, (c + d) % 16), device_id_type=MESH)
    for d in range(1, n_row):
        pl.semaphore_signal(barrier, inc=1, device_id=((r + d) % n_row, c), device_id_type=MESH)

    low16 = lower_half((16, 128))
    for a in range(2):
        for j in range(4):
            tile = panel[a, :, 128 * j : 128 * j + 128]
            top, bottom = tile[:16], tile[16:]
            pan_send[a, 2 * j] = jnp.where(low16, top, swap(bottom))
            pan_send[a, 2 * j + 1] = jnp.where(low16, swap(top), bottom)
        xy_send[a, :32, :64] = row_basis[a]
        xy_send[a, :32, 64:] = row_coeff[a]
        xy_send[a, 32:, :64] = pivot_basis[16 * a : 16 * a + 8]
        xy_send[a, 32:, 64:] = pivot_basis[16 * a + 8 : 16 * a + 16]
        zg_send[a, :, :64] = col_basis[a]
        zg_send[a, :, 64:] = col_scaled[a]
    pan_recv[c] = pan_send[k, z]
    xy[k, c] = xy_send[k]
    zg[r] = zg_send[...]
    pan_chip[k] = panel[k]

    pl.semaphore_wait(barrier, 14 + n_row)

    def copy(src, dst, send_sem, recv_sem, row, col):
        return pltpu.make_async_remote_copy(
            src_ref=src,
            dst_ref=dst,
            send_sem=send_sem,
            recv_sem=recv_sem,
            device_id=(row, col),
            device_id_type=MESH,
        )

    sends = []

    def send(*args):
        one = copy(*args)
        one.start()
        sends.append(one)

    def to_peer(i, src, dst):
        send(src, dst, peer_ss.at[i], peer_rs.at[i], r, peer)

    def from_peer(i, ref):
        copy(ref, ref, peer_ss.at[i], peer_rs.at[i], r, peer).wait_recv()

    order = [8, 9, 7, 10, 6, 11, 5, 12, 4, 13, 3, 14, 2, 15, 1]
    for d in order:
        to = (c + d) % 16
        send(pan_send.at[to % 2, to // 2], pan_recv.at[c], pan_ss.at[d], pan_rs.at[c], r, to)
    to_peer(0, panel.at[1 - k], pan_chip.at[k])
    for d in order:
        to = (c + d) % 16
        send(xy_send.at[to % 2], xy.at[to % 2, c], xy_ss.at[d], xy_rs.at[c], r, to)
    for d in range(1, n_row):
        to = (r + d) % n_row
        send(zg_send, zg.at[r], zg_ss.at[d], zg_rs.at[r], to, c)

    q_ids = lax.broadcasted_iota(jnp.int32, (512, 512), 0)
    chosen[...] = (q_ids == perm[...]).astype(F32).astype(BF16)
    t_ids = lax.broadcasted_iota(jnp.int32, (256, 512), 1)
    spread = (t_ids // 2 == lax.broadcasted_iota(jnp.int32, (256, 512), 0)).astype(F32).astype(BF16)
    values = jnp.concatenate([pivot_values[...], pair_kind[...].astype(F32), jnp.zeros((4, 256), F32)], axis=0)
    values = select_dot(values, spread, NN)
    first, second, offdiag, twin = values[0:1], values[1:2], values[2:3], values[3:4] > 0.5
    odd = lax.broadcasted_iota(jnp.int32, (1, 512), 1) % 2 == 1
    own = jnp.where(odd, second, first)
    other = jnp.where(odd, first, second)
    determinant = first * second - offdiag * offdiag
    alpha = jnp.where(twin, other / determinant, 1.0 / own)
    beta = jnp.where(twin, -offdiag / determinant, 0.0)

    def pair_apply(x):
        partner = jnp.where(odd, pltpu.roll(x, 1, 1), pltpu.roll(x, 511, 1))
        return x * alpha + partner * beta

    scaled = select_dot(pair_apply(sketch[...]), chosen[...], NT)

    for d in order:
        at = (c + d) % 16
        copy(pan_recv.at[at], pan_recv.at[at], pan_ss.at[0], pan_rs.at[at], r, at).wait_recv()
    for i in range(16):
        block = pan_recv[i]
        pan_full[32 * i : 32 * i + 16] = block
        pan_full[32 * i + 16 : 32 * i + 32] = swap(block)
    folded = fold(dot(scaled, pan_full[...]))
    rng_send[...] = folded
    rng_recv[z] = folded
    steps = [4, 5, 3, 6, 2, 7, 1]
    for d in steps:
        to = 2 * ((z + d) % 8) + k
        send(rng_send, rng_recv.at[z], rng_ss.at[d], rng_rs.at[z], r, to)

    for d in order:
        at = (c + d) % 16
        copy(xy.at[k, at], xy.at[k, at], xy_ss.at[0], xy_rs.at[at], r, at).wait_recv()
    to_peer(1, xy.at[k], xy.at[k])
    pivot_core = jnp.zeros((64, 128), F32)
    left = xy[k, :, :32].reshape(512, 128)
    pivot_core = dot(pivot_scaled[...], left)
    from_peer(0, pan_chip.at[1 - k])
    from_peer(1, xy.at[1 - k])
    for i in range(16):
        for half in range(2):
            block = xy[half, i, 32:]
            at = 32 * i + 16 * half
            basis_full[at : at + 8] = block
            basis_full[at + 8 : at + 16] = swap(block)
    weights = dot(scaled, basis_full[...])[:, :64]
    mine = basis_full[pl.ds(pl.multiple_of(64 * z, 64), 64), :][:, :64]
    mixed = dot(jnp.concatenate([weights, mine], axis=0), pivot_core)
    mixed = jnp.where(lower_half((128, 128)), swap(mixed), 0.0)
    fixes = dot(mixed, left, NT)
    updated[64:] = pan_chip[...].reshape(64, 512) - fixes[64:]

    for d in steps:
        at = (z + d) % 8
        copy(rng_recv.at[at], rng_recv.at[at], rng_ss.at[0], rng_rs.at[at], r, 2 * at + k).wait_recv()
    total = unfold(rng_recv) - fixes[:64]
    updated[:64] = total
    ranges[k] = total
    products = dot(total, updated[...], NT)
    folded = fold(swap(products))
    c_send[...] = folded
    c_recv[z] = folded
    for d in steps:
        to = 2 * ((z + d) % 8) + k
        send(c_send, c_recv.at[z], c_ss.at[d], c_rs.at[z], r, to)
    to_peer(2, ranges.at[k], ranges.at[k])

    inverses[k] = swap(inverse_factor(products[:, :64] * (1.0 / 512.0)))
    to_peer(3, inverses.at[k], inverses.at[k])

    for d in steps:
        at = (z + d) % 8
        copy(c_recv.at[at], c_recv.at[at], c_ss.at[0], c_rs.at[at], r, 2 * at + k).wait_recv()
    permuted = select_dot(unfold(c_recv), chosen[...], NN)
    coeffs[k] = pair_apply(permuted) * (512.0**-0.5)
    to_peer(4, coeffs.at[k], coeffs.at[k])

    for d in range(1, n_row):
        at = (r + d) % n_row
        copy(zg.at[at], zg.at[at], zg_ss.at[0], zg_rs.at[at], at, c).wait_recv()
    from_peer(2, ranges.at[1 - k])
    from_peer(3, inverses.at[1 - k])
    from_peer(4, coeffs.at[1 - k])
    for one in sends:
        one.wait_send()


def trail_kernel(xy, zg, ranges, coeffs, inverses, trail, trail_out, basis_out, coeff_out, lefts, rights):
    step = pl.program_id(0)

    @pl.when(step == 0)
    def _():
        low = lower_half((512, 128))
        for b in range(2):
            both = zg[:, b].reshape(512, 128)
            twice = jnp.where(low, both, swap(both))
            high = twice.astype(BF16).astype(F32)
            pair = jnp.where(low, high, twice - high).astype(BF16)
            rights[b] = jnp.concatenate([pair, pair], axis=1)
        for a in range(2):
            rows = xy[a, :, :32].reshape(512, 128)
            for b in range(2):
                both = zg[:, b].reshape(512, 128)
                core = dot(rows, both, TN)[64:, 64:]
                core = jnp.concatenate([core, core], axis=1)
                core = jnp.concatenate([core, jnp.zeros((64, 128), F32)], axis=0)
                left = dot(rows, core)
                high = left.astype(BF16)
                lefts[a, b] = jnp.concatenate([high, (left - high.astype(F32)).astype(BF16)], axis=1)
            inverse = inverses[a][:, :64]
            basis_out[a] = dot(inverse, ranges[a])
            coeff_out[a] = dot(inverse, coeffs[a])

    a = step // 4
    at = pl.multiple_of((step % 4) * 128, 128)
    for b in range(2):
        change = lax.dot_general(
            lefts[a, b, pl.ds(at, 128), :], rights[b], NT, preferred_element_type=F32
        )
        for j in range(4):
            rows = pl.ds(4 * b + j, 128, stride=8)
            trail_out[rows, :] = trail[rows, :] - change[:, 128 * j : 128 * j + 128]


def body(n_row, trail, panel, row_basis, row_coeff, col_basis, col_scaled, pivot_basis, pivot_scaled, sketch, perm, pair_kind, pivot_values):
    turn = lambda x: jnp.swapaxes(x[:, 0], 1, 2)
    dma = pltpu.SemaphoreType.DMA
    xy, zg, ranges, coeffs, inverses = pl.pallas_call(
        functools.partial(panel_kernel, n_row),
        out_shape=(
            jax.ShapeDtypeStruct((2, 16, 40, 128), F32),
            jax.ShapeDtypeStruct((n_row, 2, 32, 128), F32),
            jax.ShapeDtypeStruct((2, 64, 512), F32),
            jax.ShapeDtypeStruct((2, 64, 512), F32),
            jax.ShapeDtypeStruct((2, 64, 128), F32),
        ),
        in_specs=[VMEM] * 11,
        out_specs=(VMEM,) * 5,
        scratch_shapes=[
            pltpu.VMEM((2, 8, 16, 128), F32),
            pltpu.VMEM((16, 16, 128), F32),
            pltpu.VMEM((2, 32, 512), F32),
            pltpu.VMEM((512, 128), F32),
            pltpu.VMEM((2, 40, 128), F32),
            pltpu.VMEM((2, 32, 128), F32),
            pltpu.VMEM((32, 128), F32),
            pltpu.VMEM((8, 32, 128), F32),
            pltpu.VMEM((32, 128), F32),
            pltpu.VMEM((8, 32, 128), F32),
            pltpu.VMEM((512, 128), F32),
            pltpu.VMEM((512, 512), BF16),
            pltpu.VMEM((128, 512), F32),
            dma((16,)),
            dma((16,)),
            dma((16,)),
            dma((16,)),
            dma((n_row,)),
            dma((n_row,)),
            dma((8,)),
            dma((8,)),
            dma((8,)),
            dma((8,)),
            dma((5,)),
            dma((5,)),
        ],
        compiler_params=pltpu.CompilerParams(
            collective_id=0, has_side_effects=True, vmem_limit_bytes=24 * 1024 * 1024
        ),
        name="panel",
    )(
        turn(panel),
        turn(row_basis),
        turn(row_coeff),
        turn(col_basis),
        turn(col_scaled),
        pivot_basis.T,
        pivot_scaled,
        sketch,
        perm.reshape(1, 512),
        pair_kind.reshape(1, 256),
        pivot_values,
    )
    block = pl.BlockSpec((1024, 128), lambda i: (i, 0))
    trail_out, basis_out, coeff_out = pl.pallas_call(
        trail_kernel,
        grid=(8,),
        out_shape=(
            jax.ShapeDtypeStruct((8192, 128), F32),
            jax.ShapeDtypeStruct((2, 64, 512), F32),
            jax.ShapeDtypeStruct((2, 64, 512), F32),
        ),
        in_specs=[VMEM] * 5 + [block],
        out_specs=(block, VMEM, VMEM),
        scratch_shapes=[pltpu.VMEM((2, 2, 512, 256), BF16), pltpu.VMEM((2, 512, 256), BF16)],
        compiler_params=pltpu.CompilerParams(vmem_limit_bytes=24 * 1024 * 1024),
        name="trail",
    )(xy, zg, ranges, coeffs, inverses, trail.reshape(8192, 128))
    return (trail_out.reshape(trail.shape), basis_out[:, None], coeff_out[:, None])


def solution(mesh):
    n_row = mesh.shape["row"]
    return jax.shard_map(
        functools.partial(body, n_row),
        mesh=mesh,
        in_specs=(
            P(None, "row", None, None, "col", None),
            P(None, "row", None, "col"),
            P(None, "row", None, "col"),
            P(None, "row", None, "col"),
            P(None, "col", None, "row"),
            P(None, "col", None, "row"),
            P(None, "col"),
            P(),
            P(),
            P(),
            P(),
            P(),
        ),
        out_specs=(
            P(None, "row", None, None, "col", None),
            P(None, "row", None, None),
            P(None, "row", None, None),
        ),
        check_vma=False,
    )
```

time: 151 us -> 56.6 us (0.37)
  blocking collectives: 63.2 us -> 0 us
  Pallas kernels: 0 us -> 44.7 us
  other arithmetic: 32 us -> 0 us
  local copies, waits for them, and re-layouts: 29.1 us -> 10.7 us
  between operations: 14.4 us -> 0.67 us
  matrix products: 11.7 us -> 0 us
    all_gather x3 -> x0, blocking collectives: 63.2 us -> none  [the longest x2 42.6 us: gather_turned(): filled, at, outs = (lax.all_gather(both, axis, axis=0, tiled=True), 0, [])]
    pallas_call x0 -> x2, Pallas kernels: none -> 44.7 us  [the longest x1 37.1 us: body(): pl.pallas_call(functools.partial(panel_kernel, n_row), out_shape=(jax.Sha...]
    another operation x8 -> x0, other arithmetic: 22.1 us -> none  [the longest x4 11.9 us: body(): basis = tri_solve(jnp.linalg.cholesky(gram), range_t)]
    unnamed x18 -> x24, local copies, waits for them, and re-layouts: 23.8 us -> 10.7 us
    dot_general x10 -> x0, matrix products: 11.2 us -> none  [the longest x1 6.7 us: body(): change = jnp.einsum('apbs,bsq->apbq', left, zcols, precision=highest)]
    select_n x4 -> x0, other arithmetic: 4.99 us -> none  [the longest x2 4.37 us: pair_apply(): jnp.where(twin, (first_in * diag_two - second_in * offdiag) / determinant...]
    reduce_sum x1 -> x0, other arithmetic: 2.64 us -> none  [total_of_pieces(): return lax.all_gather(array, axis).sum(0)]
    gather x1 -> x0, local copies, waits for them, and re-layouts: 2.07 us -> none  [body(): permuted = jnp.take(projected, perm, axis=2)]
  transfers between devices with their start and end apart: 1 -> 0, of which waited for: 0 -> 0; matrix products, arithmetic and copies ran while one was open for 20% -> 0% of each run, Pallas kernels for 0% -> 0%
where the time goes in v1:
time: 56.6 us; the launch traced here: 56 us
  Pallas kernels  44.7 us (79%)
  local copies, waits for them, and re-layouts  10.7 us (19%)
  between operations  0.67 us (1%)
    pallas_call x1, Pallas kernels, body(): pl.pallas_call(functools.partial(panel_kernel, n_row), out_shape=(jax.Sha...  37.1 us
    unnamed x24, local copies, waits for them, and re-layouts  10.7 us
    pallas_call x1, Pallas kernels, body(): pl.pallas_call(trail_kernel, grid=(8,), out_shape=(jax.ShapeDtypeStruct((...  7.53 us

profile of v1, /device:TPU:1, one launch (start us, length us, event | category | flops | bytes accessed | tf_op | source)
XLA Modules:
  0.0 56.0 jit_solution(6567410629809276859)
XLA Ops:
  0.6 0.0 copy-start.1
  0.6 0.9 %copy-done.1 = f32[2,1,512,32]{2,3,1,0:T(8,128)S(1)} copy-done((f32[2,1,512,32]{2,3,1,0:T(8,128)S(1)}, f32[2,1,512,32]{2,3,1,0:T(8,128)}, u32[]{:S(2)}) %copy-start.1) | copy-done | bytes 131096
  1.5 0.0 copy-start.2
  1.5 0.9 %copy-done.2 = f32[64,512]{1,0:T(8,128)S(1)} copy-done((f32[64,512]{1,0:T(8,128)S(1)}, f32[64,512]{1,0:T(8,128)}, u32[]{:S(2)}) %copy-start.2) | copy-done | bytes 131096
  2.4 0.0 copy-start.3
  2.4 0.9 %copy-done.3 = f32[64,512]{1,0:T(8,128)S(1)} copy-done((f32[64,512]{1,0:T(8,128)S(1)}, f32[64,512]{1,0:T(8,128)}, u32[]{:S(2)}) %copy-start.3) | copy-done | bytes 131096
  3.4 0.0 copy-start.4
  3.4 0.8 %copy-done.4 = f32[2,1,64,32]{2,3,1,0:T(8,128)S(1)} copy-done((f32[2,1,64,32]{2,3,1,0:T(8,128)S(1)}, f32[2,1,64,32]{2,3,1,0:T(8,128)}, u32[]{:S(2)}) %copy-start.4) | copy-done | bytes 16408
  4.1 0.0 copy-start.5
  4.1 0.8 %copy-done.5 = f32[2,1,64,32]{2,3,1,0:T(8,128)S(1)} copy-done((f32[2,1,64,32]{2,3,1,0:T(8,128)S(1)}, f32[2,1,64,32]{2,3,1,0:T(8,128)}, u32[]{:S(2)}) %copy-start.5) | copy-done | bytes 16408
  4.9 0.0 copy-start.6
  4.9 0.8 %copy-done.6 = f32[2,1,64,32]{2,3,1,0:T(8,128)S(1)} copy-done((f32[2,1,64,32]{2,3,1,0:T(8,128)S(1)}, f32[2,1,64,32]{2,3,1,0:T(8,128)}, u32[]{:S(2)}) %copy-start.6) | copy-done | bytes 16408
  5.6 0.0 copy-start.7
  5.6 0.8 %copy-done.7 = f32[2,1,64,32]{2,3,1,0:T(8,128)S(1)} copy-done((f32[2,1,64,32]{2,3,1,0:T(8,128)S(1)}, f32[2,1,64,32]{2,3,1,0:T(8,128)}, u32[]{:S(2)}) %copy-start.7) | copy-done | bytes 16408
  6.4 0.0 copy-start.8
  6.4 0.7 %copy-done.8 = f32[64,32]{0,1:T(8,128)S(1)} copy-done((f32[64,32]{0,1:T(8,128)S(1)}, f32[64,32]{0,1:T(8,128)}, u32[]{:S(2)}) %copy-start.8) | copy-done | bytes 8216
  7.1 0.0 copy-start.9
  7.1 0.7 %copy-done.9 = f32[3,256]{1,0:T(4,128)S(1)} copy-done((f32[3,256]{1,0:T(4,128)S(1)}, f32[3,256]{1,0:T(4,128)}, u32[]{:S(2)}) %copy-start.9) | copy-done | bytes 3096
  7.8 0.0 copy-start.10
  7.8 0.7 %copy-done.10 = s32[512]{0:T(512)S(1)} copy-done((s32[512]{0:T(512)S(1)}, s32[512]{0:T(512)}, u32[]{:S(2)}) %copy-start.10) | copy-done | bytes 2072
  8.5 0.0 copy-start.11
  8.5 0.7 %copy-done.11 = s32[256]{0:T(256)S(1)} copy-done((s32[256]{0:T(256)S(1)}, s32[256]{0:T(256)}, u32[]{:S(2)}) %copy-start.11) | copy-done | bytes 1048
  9.2 37.1 %panel.1 = (f32[2,16,40,128]{3,2,1,0:T(8,128)S(1)}, f32[16,2,32,128]{3,2,1,0:T(8,128)S(1)}, f32[2,64,512]{2,1,0:T(8,128)S(1)}, f32[2,64,512]{2,1,0:T(8,128)S(1)}, f32[2,64,128]{2,1,0:T(8,128)S(1)}) custom-call(f32[2,32,512]{2,1,0:T(8,128)S(1)} %bitcast.27, f32[2,32,64]{2,1,0:T(8,128)S(1)} %bitcast.28, f32[2,32,64]{2,1,0:T(8,128)S(1)} %bitcast.29, ...), custom_call_target="tpu_custom_call" | custom-call | tf_op jit(solution)/shard_map/panel/pallas_call | solution.py:338
  46.3 0.0 copy-start
  46.3 2.2 %copy-done = f32[2,1,512,2,1,512]{5,4,3,2,1,0:T(1,128)S(1)} copy-done((f32[2,1,512,2,1,512]{5,4,3,2,1,0:T(1,128)S(1)}, f32[2,1,512,2,1,512]{5,4,3,2,1,0:T(1,128)}, u32[]{:S(2)}) %copy-start) | copy-done | bytes 4194328
  48.5 7.5 %trail.1 = (f32[8192,128]{1,0:T(8,128)}, f32[2,64,512]{2,1,0:T(8,128)}, f32[2,64,512]{2,1,0:T(8,128)}) custom-call(f32[2,16,40,128]{3,2,1,0:T(8,128)S(1)} %get-tuple-element.11.xy, f32[16,2,32,128]{3,2,1,0:T(8,128)S(1)} %get-tuple-element.12.zg, f32[2,64,512]{2,1,0:T(8,128)S(1)} %get-tuple-element.13.ranges, f32[2,64,512]{2,1,0:T(8,128)S(1)} %get-tuple-element.14.coeffs, ...), custom_call_target="tpu_custom_call" | custom-call | tf_op jit(solution)/shard_map/trail/pallas_call | solution.py:394
Async XLA Ops:
  0.6 0.9 %copy-start.1 = (f32[2,1,512,32]{2,3,1,0:T(8,128)S(1)}, f32[2,1,512,32]{2,3,1,0:T(8,128)}, u32[]{:S(2)}) copy-start(f32[2,1,512,32]{2,3,1,0:T(8,128)} %param.13) | copy-start | bytes 393220
  1.5 0.9 %copy-start.2 = (f32[64,512]{1,0:T(8,128)S(1)}, f32[64,512]{1,0:T(8,128)}, u32[]{:S(2)}) copy-start(f32[64,512]{1,0:T(8,128)} %pivot_scaled.1) | copy-start | bytes 393220
  2.4 0.9 %copy-start.3 = (f32[64,512]{1,0:T(8,128)S(1)}, f32[64,512]{1,0:T(8,128)}, u32[]{:S(2)}) copy-start(f32[64,512]{1,0:T(8,128)} %sketch.1) | copy-start | bytes 393220
  3.4 0.8 %copy-start.4 = (f32[2,1,64,32]{2,3,1,0:T(8,128)S(1)}, f32[2,1,64,32]{2,3,1,0:T(8,128)}, u32[]{:S(2)}) copy-start(f32[2,1,64,32]{2,3,1,0:T(8,128)} %param.14) | copy-start | bytes 49156
  4.1 0.8 %copy-start.5 = (f32[2,1,64,32]{2,3,1,0:T(8,128)S(1)}, f32[2,1,64,32]{2,3,1,0:T(8,128)}, u32[]{:S(2)}) copy-start(f32[2,1,64,32]{2,3,1,0:T(8,128)} %param.15) | copy-start | bytes 49156
  4.9 0.8 %copy-start.6 = (f32[2,1,64,32]{2,3,1,0:T(8,128)S(1)}, f32[2,1,64,32]{2,3,1,0:T(8,128)}, u32[]{:S(2)}) copy-start(f32[2,1,64,32]{2,3,1,0:T(8,128)} %param.16) | copy-start | bytes 49156
  5.6 0.8 %copy-start.7 = (f32[2,1,64,32]{2,3,1,0:T(8,128)S(1)}, f32[2,1,64,32]{2,3,1,0:T(8,128)}, u32[]{:S(2)}) copy-start(f32[2,1,64,32]{2,3,1,0:T(8,128)} %param.17) | copy-start | bytes 49156
  6.4 0.7 %copy-start.8 = (f32[64,32]{0,1:T(8,128)S(1)}, f32[64,32]{0,1:T(8,128)}, u32[]{:S(2)}) copy-start(f32[64,32]{0,1:T(8,128)} %param.18) | copy-start | bytes 24580
  7.1 0.7 %copy-start.9 = (f32[3,256]{1,0:T(4,128)S(1)}, f32[3,256]{1,0:T(4,128)}, u32[]{:S(2)}) copy-start(f32[3,256]{1,0:T(4,128)} %pivot_values.1) | copy-start | bytes 9220
  7.8 0.7 %copy-start.10 = (s32[512]{0:T(512)S(1)}, s32[512]{0:T(512)}, u32[]{:S(2)}) copy-start(s32[512]{0:T(512)} %param.21) | copy-start | bytes 6148
  8.5 0.7 %copy-start.11 = (s32[256]{0:T(256)S(1)}, s32[256]{0:T(256)}, u32[]{:S(2)}) copy-start(s32[256]{0:T(256)} %param.22) | copy-start | bytes 3076
  46.3 2.2 %copy-start = (f32[2,1,512,2,1,512]{5,4,3,2,1,0:T(1,128)S(1)}, f32[2,1,512,2,1,512]{5,4,3,2,1,0:T(1,128)}, u32[]{:S(2)}) copy-start(f32[2,1,512,2,1,512]{5,4,3,2,1,0:T(1,128)} %param.12) | copy-start | bytes 12582916

commit v2 on v1

--- a/solution.py
+++ b/solution.py
@@ -15,6 +15,7 @@
 NT = (((1,), (1,)), ((), ()))
 TN = (((0,), (0,)), ((), ()))
 VMEM = pl.BlockSpec(memory_space=pltpu.VMEM)
+HBM = pl.BlockSpec(memory_space=pltpu.HBM)
 
 
 def dot(a, b, dims=NN):
@@ -94,22 +95,24 @@
 
 def panel_kernel(
     n_row,
-    panel,
-    row_basis,
-    row_coeff,
-    col_basis,
-    col_scaled,
-    pivot_basis,
-    pivot_scaled,
-    sketch,
-    perm,
-    pair_kind,
-    pivot_values,
-    xy,
-    zg,
+    trail_hbm,
+    *refs,
+):
+    inputs, refs = refs[:11], refs[11:]
+    run_panel(n_row, trail_hbm, inputs, *refs)
+
+
+def run_panel(
+    n_row,
+    trail_hbm,
+    inputs,
+    trail,
     ranges,
     coeffs,
     inverses,
+    xy,
+    zg,
+    staged,
     pan_send,
     pan_recv,
     pan_chip,
@@ -135,6 +138,10 @@
     c_rs,
     peer_ss,
     peer_rs,
+    in_sem,
+    trail_sem,
+    lefts,
+    rights,
 ):
     r = lax.axis_index("row")
     c = lax.axis_index("col")
@@ -142,12 +149,20 @@
     k = c % 2
     peer = 2 * z + 1 - k
 
+    loads = [pltpu.make_async_copy(src, dst, in_sem.at[i]) for i, (src, dst) in enumerate(zip(inputs, staged))]
+    for one in loads:
+        one.start()
+    trail_load = pltpu.make_async_copy(trail_hbm, trail, trail_sem)
+    panel, row_basis, row_coeff, pivot_basis, col_basis, col_scaled, sketch, perm, pair_kind, pivot_values, pivot_scaled = staged
+
     barrier = pltpu.get_barrier_semaphore()
     for d in range(1, 16):
         pl.semaphore_signal(barrier, inc=1, device_id=(r, (c + d) % 16), device_id_type=MESH)
     for d in range(1, n_row):
         pl.semaphore_signal(barrier, inc=1, device_id=((r + d) % n_row, c), device_id_type=MESH)
 
+    for one in loads:
+        one.wait()
     low16 = lower_half((16, 128))
     for a in range(2):
         for j in range(4):
@@ -203,6 +218,7 @@
         to = (r + d) % n_row
         send(zg_send, zg.at[r], zg_ss.at[d], zg_rs.at[r], to, c)
 
+    trail_load.start()
     q_ids = lax.broadcasted_iota(jnp.int32, (512, 512), 0)
     chosen[...] = (q_ids == perm[...]).astype(F32).astype(BF16)
     t_ids = lax.broadcasted_iota(jnp.int32, (256, 512), 1)
@@ -242,7 +258,6 @@
         at = (c + d) % 16
         copy(xy.at[k, at], xy.at[k, at], xy_ss.at[0], xy_rs.at[at], r, at).wait_recv()
     to_peer(1, xy.at[k], xy.at[k])
-    pivot_core = jnp.zeros((64, 128), F32)
     left = xy[k, :, :32].reshape(512, 128)
     pivot_core = dot(pivot_scaled[...], left)
     from_peer(0, pan_chip.at[1 - k])
@@ -275,8 +290,43 @@
         send(c_send, c_recv.at[z], c_ss.at[d], c_rs.at[z], r, to)
     to_peer(2, ranges.at[k], ranges.at[k])
 
+    for d in range(1, n_row):
+        at = (r + d) % n_row
+        copy(zg.at[at], zg.at[at], zg_ss.at[0], zg_rs.at[at], at, c).wait_recv()
+    trail_load.wait()
     inverses[k] = swap(inverse_factor(products[:, :64] * (1.0 / 512.0)))
     to_peer(3, inverses.at[k], inverses.at[k])
+    low = lower_half((512, 128))
+    columns = []
+    for b in range(2):
+        both = zg[:, b].reshape(512, 128)
+        columns.append(both)
+        twice = jnp.where(low, both, swap(both))
+        high = twice.astype(BF16).astype(F32)
+        pair = jnp.where(low, high, twice - high).astype(BF16)
+        rights[b] = jnp.concatenate([pair, pair], axis=1)
+    columns = jnp.concatenate(columns, axis=1)
+    for a in range(2):
+        rows = xy[a, :, :32].reshape(512, 128)
+        cores = dot(rows, columns, TN)[64:]
+        low = lower_half((64, 128))
+        cores = [jnp.where(low, swap(core), core) for core in (cores[:, :128], cores[:, 128:])]
+        cores = jnp.concatenate([jnp.concatenate(cores, axis=1), jnp.zeros((64, 256), F32)], axis=0)
+        left = dot(rows, cores)
+        high = left.astype(BF16)
+        rest = (left - high.astype(F32)).astype(BF16)
+        for b in range(2):
+            lefts[a, b, :, :128] = high[:, 128 * b : 128 * b + 128]
+            lefts[a, b, :, 128:] = rest[:, 128 * b : 128 * b + 128]
+    for a in range(2):
+        for part in range(4):
+            for b in range(2):
+                change = lax.dot_general(
+                    lefts[a, b, 128 * part : 128 * part + 128], rights[b], NT, preferred_element_type=F32
+                )
+                for j in range(4):
+                    lines = pl.ds(4096 * a + 1024 * part + 4 * b + j, 128, stride=8)
+                    trail[lines, :] = trail[lines, :] - change[:, 128 * j : 128 * j + 128]
 
     for d in steps:
         at = (z + d) % 8
@@ -285,9 +335,6 @@
     coeffs[k] = pair_apply(permuted) * (512.0**-0.5)
     to_peer(4, coeffs.at[k], coeffs.at[k])
 
-    for d in range(1, n_row):
-        at = (r + d) % n_row
-        copy(zg.at[at], zg.at[at], zg_ss.at[0], zg_rs.at[at], at, c).wait_recv()
     from_peer(2, ranges.at[1 - k])
     from_peer(3, inverses.at[1 - k])
     from_peer(4, coeffs.at[1 - k])
@@ -295,58 +342,52 @@
         one.wait_send()
 
 
-def trail_kernel(xy, zg, ranges, coeffs, inverses, trail, trail_out, basis_out, coeff_out, lefts, rights):
-    step = pl.program_id(0)
-
-    @pl.when(step == 0)
-    def _():
-        low = lower_half((512, 128))
-        for b in range(2):
-            both = zg[:, b].reshape(512, 128)
-            twice = jnp.where(low, both, swap(both))
-            high = twice.astype(BF16).astype(F32)
-            pair = jnp.where(low, high, twice - high).astype(BF16)
-            rights[b] = jnp.concatenate([pair, pair], axis=1)
-        for a in range(2):
-            rows = xy[a, :, :32].reshape(512, 128)
-            for b in range(2):
-                both = zg[:, b].reshape(512, 128)
-                core = dot(rows, both, TN)[64:, 64:]
-                core = jnp.concatenate([core, core], axis=1)
-                core = jnp.concatenate([core, jnp.zeros((64, 128), F32)], axis=0)
-                left = dot(rows, core)
-                high = left.astype(BF16)
-                lefts[a, b] = jnp.concatenate([high, (left - high.astype(F32)).astype(BF16)], axis=1)
-            inverse = inverses[a][:, :64]
-            basis_out[a] = dot(inverse, ranges[a])
-            coeff_out[a] = dot(inverse, coeffs[a])
-
-    a = step // 4
-    at = pl.multiple_of((step % 4) * 128, 128)
-    for b in range(2):
-        change = lax.dot_general(
-            lefts[a, b, pl.ds(at, 128), :], rights[b], NT, preferred_element_type=F32
-        )
-        for j in range(4):
-            rows = pl.ds(4 * b + j, 128, stride=8)
-            trail_out[rows, :] = trail[rows, :] - change[:, 128 * j : 128 * j + 128]
+def finish_kernel(trail, ranges, coeffs, inverses, trail_out, basis_out, coeff_out, basis, coeff, sems):
+    copies = [pltpu.make_async_copy(trail.at[pl.ds(2048 * i, 2048)], trail_out.at[pl.ds(2048 * i, 2048)], sems.at[i]) for i in range(4)]
+    for one in copies:
+        one.start()
+    for a in range(2):
+        inverse = inverses[a][:, :64]
+        basis[a] = dot(inverse, ranges[a])
+        coeff[a] = dot(inverse, coeffs[a])
+    copies += [pltpu.make_async_copy(basis, basis_out, sems.at[4]), pltpu.make_async_copy(coeff, coeff_out, sems.at[5])]
+    for one in copies[4:]:
+        one.start()
+    for one in copies:
+        one.wait()
 
 
 def body(n_row, trail, panel, row_basis, row_coeff, col_basis, col_scaled, pivot_basis, pivot_scaled, sketch, perm, pair_kind, pivot_values):
     turn = lambda x: jnp.swapaxes(x[:, 0], 1, 2)
     dma = pltpu.SemaphoreType.DMA
-    xy, zg, ranges, coeffs, inverses = pl.pallas_call(
+    inputs = (
+        turn(panel),
+        turn(row_basis),
+        turn(row_coeff),
+        pivot_basis.T,
+        turn(col_basis),
+        turn(col_scaled),
+        sketch,
+        perm.reshape(1, 512),
+        pair_kind.reshape(1, 256),
+        pivot_values,
+        pivot_scaled,
+    )
+    small = jax.ShapeDtypeStruct((2, 64, 512), F32)
+    results = pl.pallas_call(
         functools.partial(panel_kernel, n_row),
         out_shape=(
-            jax.ShapeDtypeStruct((2, 16, 40, 128), F32),
-            jax.ShapeDtypeStruct((n_row, 2, 32, 128), F32),
-            jax.ShapeDtypeStruct((2, 64, 512), F32),
-            jax.ShapeDtypeStruct((2, 64, 512), F32),
+            jax.ShapeDtypeStruct((8192, 128), F32),
+            small,
+            small,
             jax.ShapeDtypeStruct((2, 64, 128), F32),
         ),
-        in_specs=[VMEM] * 11,
-        out_specs=(VMEM,) * 5,
+        in_specs=[HBM] * 12,
+        out_specs=(VMEM,) * 4,
         scratch_shapes=[
+            pltpu.VMEM((2, 16, 40, 128), F32),
+            pltpu.VMEM((n_row, 2, 32, 128), F32),
+            [pltpu.VMEM(x.shape, x.dtype) for x in inputs],
             pltpu.VMEM((2, 8, 16, 128), F32),
             pltpu.VMEM((16, 16, 128), F32),
             pltpu.VMEM((2, 32, 512), F32),
@@ -372,39 +413,25 @@
             dma((8,)),
             dma((5,)),
             dma((5,)),
+            dma((11,)),
+            dma(()),
+            pltpu.VMEM((2, 2, 512, 256), BF16),
+            pltpu.VMEM((2, 512, 256), BF16),
         ],
         compiler_params=pltpu.CompilerParams(
-            collective_id=0, has_side_effects=True, vmem_limit_bytes=24 * 1024 * 1024
+            collective_id=0, has_side_effects=True, vmem_limit_bytes=40 * 1024 * 1024
         ),
         name="panel",
-    )(
-        turn(panel),
-        turn(row_basis),
-        turn(row_coeff),
-        turn(col_basis),
-        turn(col_scaled),
-        pivot_basis.T,
-        pivot_scaled,
-        sketch,
-        perm.reshape(1, 512),
-        pair_kind.reshape(1, 256),
-        pivot_values,
-    )
-    block = pl.BlockSpec((1024, 128), lambda i: (i, 0))
+    )(*[pltpu.with_memory_space_constraint(x, pltpu.HBM) for x in (trail.reshape(8192, 128), *inputs)])
     trail_out, basis_out, coeff_out = pl.pallas_call(
-        trail_kernel,
-        grid=(8,),
-        out_shape=(
-            jax.ShapeDtypeStruct((8192, 128), F32),
-            jax.ShapeDtypeStruct((2, 64, 512), F32),
-            jax.ShapeDtypeStruct((2, 64, 512), F32),
-        ),
-        in_specs=[VMEM] * 5 + [block],
-        out_specs=(block, VMEM, VMEM),
-        scratch_shapes=[pltpu.VMEM((2, 2, 512, 256), BF16), pltpu.VMEM((2, 512, 256), BF16)],
-        compiler_params=pltpu.CompilerParams(vmem_limit_bytes=24 * 1024 * 1024),
-        name="trail",
-    )(xy, zg, ranges, coeffs, inverses, trail.reshape(8192, 128))
+        finish_kernel,
+        out_shape=(jax.ShapeDtypeStruct((8192, 128), F32), small, small),
+        in_specs=[VMEM] * 4,
+        out_specs=(HBM,) * 3,
+        scratch_shapes=[pltpu.VMEM((2, 64, 512), F32), pltpu.VMEM((2, 64, 512), F32), dma((6,))],
+        compiler_params=pltpu.CompilerParams(vmem_limit_bytes=40 * 1024 * 1024),
+        name="finish",
+    )(*results)
     return (trail_out.reshape(trail.shape), basis_out[:, None], coeff_out[:, None])
 
 

time: 56.6 us -> 39.1 us (0.69)
  local copies, waits for them, and re-layouts: 10.7 us -> 0 us
  Pallas kernels: 44.7 us -> 38.4 us
    unnamed x24 -> x0, local copies, waits for them, and re-layouts: 10.7 us -> none
    pallas_call x1, Pallas kernels: 7.53 us -> 2.22 us  [body(): pl.pallas_call(finish_kernel, out_shape=(jax.ShapeDtypeStruct((8192, 128)...]
    pallas_call x1, Pallas kernels: 37.1 us -> 36.2 us  [body(): pl.pallas_call(functools.partial(panel_kernel, n_row), out_shape=(jax.Sha...]
where the time goes in v2:
time: 39.1 us; the launch traced here: 39 us
  Pallas kernels  38.4 us (98%)
  between operations  0.64 us (2%)
    pallas_call x1, Pallas kernels, body(): pl.pallas_call(functools.partial(panel_kernel, n_row), out_shape=(jax.Sha...  36.2 us
    pallas_call x1, Pallas kernels, body(): pl.pallas_call(finish_kernel, out_shape=(jax.ShapeDtypeStruct((8192, 128)...  2.22 us

profile of v2, /device:TPU:1, one launch (start us, length us, event | category | flops | bytes accessed | tf_op | source)
XLA Modules:
  0.0 39.0 jit_solution(14944150579082468908)
XLA Ops:
  0.6 36.2 %panel.1 = (f32[8192,128]{1,0:T(8,128)S(1)}, f32[2,64,512]{2,1,0:T(8,128)S(1)}, f32[2,64,512]{2,1,0:T(8,128)S(1)}, f32[2,64,128]{2,1,0:T(8,128)S(1)}) custom-call(f32[8192,128]{1,0:T(8,128)} %bitcast.26, f32[2,32,512]{2,1,0:T(8,128)} %bitcast.27, f32[2,32,64]{2,1,0:T(8,128)} %bitcast.28, f32[2,32,64]{2,1,0:T(8,128)} %bitcast.29, f32[32,64]{1,0:T(8,128)} %bitcast.32, ...), custom_call_target="tpu_custom_call" | custom-call | tf_op jit(solution)/shard_map/panel/pallas_call | solution.py:377
  36.8 2.2 %finish.1 = (f32[8192,128]{1,0:T(8,128)}, f32[2,64,512]{2,1,0:T(8,128)}, f32[2,64,512]{2,1,0:T(8,128)}) custom-call(f32[8192,128]{1,0:T(8,128)S(1)} %get-tuple-element.10.trail, f32[2,64,512]{2,1,0:T(8,128)S(1)} %get-tuple-element.11.ranges, f32[2,64,512]{2,1,0:T(8,128)S(1)} %get-tuple-element.12.coeffs, f32[2,64,128]{2,1,0:T(8,128)S(1)} %get-tuple-element.13.inverses), custom_call_target="tpu_custom_call" | custom-call | tf_op jit(solution)/shard_map/finish/pallas_call | solution.py:426

commit v3 on v2

--- a/solution.py
+++ b/solution.py
@@ -28,6 +28,15 @@
     mid = rest.astype(BF16)
     low = (rest - mid.astype(F32)).astype(BF16)
     return jnp.concatenate([high, mid, low], axis=0)
+
+
+def split2(x):
+    high = x.astype(BF16)
+    return high, (x - high.astype(F32)).astype(BF16)
+
+
+def bdot(a, b, dims=NN):
+    return lax.dot_general(a, b, dims, preferred_element_type=F32)
 
 
 def select_dot(x, chosen, dims):
@@ -111,6 +120,7 @@
     coeffs,
     inverses,
     xy,
+    pb,
     zg,
     staged,
     pan_send,
@@ -118,6 +128,7 @@
     pan_chip,
     pan_full,
     xy_send,
+    pb_send,
     zg_send,
     rng_send,
     rng_recv,
@@ -130,8 +141,12 @@
     pan_rs,
     xy_ss,
     xy_rs,
-    zg_ss,
-    zg_rs,
+    pb_ss,
+    pb_rs,
+    zx_ss,
+    zx_rs,
+    zy_ss,
+    zy_rs,
     rng_ss,
     rng_rs,
     c_ss,
@@ -149,17 +164,20 @@
     k = c % 2
     peer = 2 * z + 1 - k
 
+    y, x = r // 4, r % 4
+    order = [8, 9, 7, 10, 6, 11, 5, 12, 4, 13, 3, 14, 2, 15, 1]
+
+    barrier = pltpu.get_barrier_semaphore()
+    for d in order:
+        pl.semaphore_signal(barrier, inc=1, device_id=(r, (c + d) % 16), device_id_type=MESH)
+    for d in (2, 1, 3):
+        pl.semaphore_signal(barrier, inc=1, device_id=(4 * y + (x + d) % 4, c), device_id_type=MESH)
+        pl.semaphore_signal(barrier, inc=1, device_id=(4 * ((y + d) % 4) + x, c), device_id_type=MESH)
     loads = [pltpu.make_async_copy(src, dst, in_sem.at[i]) for i, (src, dst) in enumerate(zip(inputs, staged))]
     for one in loads:
         one.start()
     trail_load = pltpu.make_async_copy(trail_hbm, trail, trail_sem)
     panel, row_basis, row_coeff, pivot_basis, col_basis, col_scaled, sketch, perm, pair_kind, pivot_values, pivot_scaled = staged
-
-    barrier = pltpu.get_barrier_semaphore()
-    for d in range(1, 16):
-        pl.semaphore_signal(barrier, inc=1, device_id=(r, (c + d) % 16), device_id_type=MESH)
-    for d in range(1, n_row):
-        pl.semaphore_signal(barrier, inc=1, device_id=((r + d) % n_row, c), device_id_type=MESH)
 
     for one in loads:
         one.wait()
@@ -170,18 +188,19 @@
             top, bottom = tile[:16], tile[16:]
             pan_send[a, 2 * j] = jnp.where(low16, top, swap(bottom))
             pan_send[a, 2 * j + 1] = jnp.where(low16, swap(top), bottom)
-        xy_send[a, :32, :64] = row_basis[a]
-        xy_send[a, :32, 64:] = row_coeff[a]
-        xy_send[a, 32:, :64] = pivot_basis[16 * a : 16 * a + 8]
-        xy_send[a, 32:, 64:] = pivot_basis[16 * a + 8 : 16 * a + 16]
+        xy_send[a, :, :64] = row_basis[a]
+        xy_send[a, :, 64:] = row_coeff[a]
+        pb_send[a, :, :64] = pivot_basis[16 * a : 16 * a + 8]
+        pb_send[a, :, 64:] = pivot_basis[16 * a + 8 : 16 * a + 16]
         zg_send[a, :, :64] = col_basis[a]
         zg_send[a, :, 64:] = col_scaled[a]
     pan_recv[c] = pan_send[k, z]
     xy[k, c] = xy_send[k]
+    pb[k, c] = pb_send[k]
     zg[r] = zg_send[...]
     pan_chip[k] = panel[k]
 
-    pl.semaphore_wait(barrier, 14 + n_row)
+    pl.semaphore_wait(barrier, 21)
 
     def copy(src, dst, send_sem, recv_sem, row, col):
         return pltpu.make_async_remote_copy(
@@ -206,17 +225,18 @@
     def from_peer(i, ref):
         copy(ref, ref, peer_ss.at[i], peer_rs.at[i], r, peer).wait_recv()
 
-    order = [8, 9, 7, 10, 6, 11, 5, 12, 4, 13, 3, 14, 2, 15, 1]
     for d in order:
         to = (c + d) % 16
         send(pan_send.at[to % 2, to // 2], pan_recv.at[c], pan_ss.at[d], pan_rs.at[c], r, to)
+    for d in (2, 1, 3):
+        send(zg_send, zg.at[r], zx_ss.at[d], zx_rs.at[x], 4 * y + (x + d) % 4, c)
+    for d in order:
+        to = (c + d) % 16
+        send(pb_send.at[to % 2], pb.at[to % 2, c], pb_ss.at[d], pb_rs.at[c], r, to)
     to_peer(0, panel.at[1 - k], pan_chip.at[k])
     for d in order:
         to = (c + d) % 16
         send(xy_send.at[to % 2], xy.at[to % 2, c], xy_ss.at[d], xy_rs.at[c], r, to)
-    for d in range(1, n_row):
-        to = (r + d) % n_row
-        send(zg_send, zg.at[r], zg_ss.at[d], zg_rs.at[r], to, c)
 
     trail_load.start()
     q_ids = lax.broadcasted_iota(jnp.int32, (512, 512), 0)
@@ -239,6 +259,12 @@
 
     scaled = select_dot(pair_apply(sketch[...]), chosen[...], NT)
 
+    mine = pl.ds(pl.multiple_of(4 * y, 4), 4)
+    for d in range(1, 4):
+        at = (x + d) % 4
+        copy(zg.at[4 * y + at], zg.at[4 * y + at], zx_ss.at[0], zx_rs.at[at], 4 * y + at, c).wait_recv()
+    for d in (2, 1, 3):
+        send(zg.at[mine], zg.at[mine], zy_ss.at[d], zy_rs.at[y], 4 * ((y + d) % 4) + x, c)
     for d in order:
         at = (c + d) % 16
         copy(pan_recv.at[at], pan_recv.at[at], pan_ss.at[0], pan_rs.at[at], r, at).wait_recv()
@@ -256,21 +282,25 @@
 
     for d in order:
         at = (c + d) % 16
-        copy(xy.at[k, at], xy.at[k, at], xy_ss.at[0], xy_rs.at[at], r, at).wait_recv()
-    to_peer(1, xy.at[k], xy.at[k])
-    left = xy[k, :, :32].reshape(512, 128)
-    pivot_core = dot(pivot_scaled[...], left)
+        copy(pb.at[k, at], pb.at[k, at], pb_ss.at[0], pb_rs.at[at], r, at).wait_recv()
+    to_peer(5, pb.at[k], pb.at[k])
     from_peer(0, pan_chip.at[1 - k])
-    from_peer(1, xy.at[1 - k])
+    from_peer(5, pb.at[1 - k])
     for i in range(16):
         for half in range(2):
-            block = xy[half, i, 32:]
+            block = pb[half, i]
             at = 32 * i + 16 * half
             basis_full[at : at + 8] = block
             basis_full[at + 8 : at + 16] = swap(block)
     weights = dot(scaled, basis_full[...])[:, :64]
     mine = basis_full[pl.ds(pl.multiple_of(64 * z, 64), 64), :][:, :64]
-    mixed = dot(jnp.concatenate([weights, mine], axis=0), pivot_core)
+    mixer = dot(jnp.concatenate([weights, mine], axis=0), pivot_scaled[...])
+    for d in order:
+        at = (c + d) % 16
+        copy(xy.at[k, at], xy.at[k, at], xy_ss.at[0], xy_rs.at[at], r, at).wait_recv()
+    to_peer(1, xy.at[k], xy.at[k])
+    left = xy[k].reshape(512, 128)
+    mixed = dot(mixer, left)
     mixed = jnp.where(lower_half((128, 128)), swap(mixed), 0.0)
     fixes = dot(mixed, left, NT)
     updated[64:] = pan_chip[...].reshape(64, 512) - fixes[64:]
@@ -290,12 +320,14 @@
         send(c_send, c_recv.at[z], c_ss.at[d], c_rs.at[z], r, to)
     to_peer(2, ranges.at[k], ranges.at[k])
 
-    for d in range(1, n_row):
-        at = (r + d) % n_row
-        copy(zg.at[at], zg.at[at], zg_ss.at[0], zg_rs.at[at], at, c).wait_recv()
-    trail_load.wait()
     inverses[k] = swap(inverse_factor(products[:, :64] * (1.0 / 512.0)))
     to_peer(3, inverses.at[k], inverses.at[k])
+    from_peer(1, xy.at[1 - k])
+    for d in range(1, 4):
+        at = (y + d) % 4
+        part = pl.ds(pl.multiple_of(4 * at, 4), 4)
+        copy(zg.at[part], zg.at[part], zy_ss.at[0], zy_rs.at[at], 4 * at + x, c).wait_recv()
+    trail_load.wait()
     low = lower_half((512, 128))
     columns = []
     for b in range(2):
@@ -305,28 +337,33 @@
         high = twice.astype(BF16).astype(F32)
         pair = jnp.where(low, high, twice - high).astype(BF16)
         rights[b] = jnp.concatenate([pair, pair], axis=1)
-    columns = jnp.concatenate(columns, axis=1)
+    columns_high, columns_low = split2(jnp.concatenate(columns, axis=1))
+    rows_high, rows_low = split2(jnp.concatenate([xy[0].reshape(512, 128), xy[1].reshape(512, 128)], axis=1))
+    cores = bdot(rows_high, columns_low, TN) + bdot(rows_low, columns_high, TN) + bdot(rows_high, columns_high, TN)
+    low = lower_half((64, 128))
     for a in range(2):
-        rows = xy[a, :, :32].reshape(512, 128)
-        cores = dot(rows, columns, TN)[64:]
-        low = lower_half((64, 128))
-        cores = [jnp.where(low, swap(core), core) for core in (cores[:, :128], cores[:, 128:])]
-        cores = jnp.concatenate([jnp.concatenate(cores, axis=1), jnp.zeros((64, 256), F32)], axis=0)
-        left = dot(rows, cores)
-        high = left.astype(BF16)
-        rest = (left - high.astype(F32)).astype(BF16)
+        core = cores[128 * a + 64 : 128 * a + 128]
+        core = [jnp.where(low, swap(half), half) for half in (core[:, :128], core[:, 128:])]
+        core = jnp.concatenate([jnp.concatenate(core, axis=1), jnp.zeros((64, 256), F32)], axis=0)
+        core_high, core_low = split2(core)
+        high, rest = rows_high[:, 128 * a : 128 * a + 128], rows_low[:, 128 * a : 128 * a + 128]
+        left = bdot(high, core_low) + bdot(
+            jnp.concatenate([high, rest], axis=1), jnp.concatenate([core_high, core_high], axis=0)
+        )
+        high, rest = split2(left)
         for b in range(2):
             lefts[a, b, :, :128] = high[:, 128 * b : 128 * b + 128]
             lefts[a, b, :, 128:] = rest[:, 128 * b : 128 * b + 128]
-    for a in range(2):
-        for part in range(4):
-            for b in range(2):
-                change = lax.dot_general(
-                    lefts[a, b, 128 * part : 128 * part + 128], rights[b], NT, preferred_element_type=F32
-                )
-                for j in range(4):
-                    lines = pl.ds(4096 * a + 1024 * part + 4 * b + j, 128, stride=8)
-                    trail[lines, :] = trail[lines, :] - change[:, 128 * j : 128 * j + 128]
+
+    def change(a, part):
+        for b in range(2):
+            delta = bdot(lefts[a, b, 128 * part : 128 * part + 128], rights[b], NT)
+            for j in range(4):
+                lines = pl.ds(4096 * a + 1024 * part + 4 * b + j, 128, stride=8)
+                trail[lines, :] = trail[lines, :] - delta[:, 128 * j : 128 * j + 128]
+
+    for part in range(4):
+        change(0, part)
 
     for d in steps:
         at = (z + d) % 8
@@ -334,6 +371,8 @@
     permuted = select_dot(unfold(c_recv), chosen[...], NN)
     coeffs[k] = pair_apply(permuted) * (512.0**-0.5)
     to_peer(4, coeffs.at[k], coeffs.at[k])
+    for part in range(4):
+        change(1, part)
 
     from_peer(2, ranges.at[1 - k])
     from_peer(3, inverses.at[1 - k])
@@ -385,14 +424,16 @@
         in_specs=[HBM] * 12,
         out_specs=(VMEM,) * 4,
         scratch_shapes=[
-            pltpu.VMEM((2, 16, 40, 128), F32),
+            pltpu.VMEM((2, 16, 32, 128), F32),
+            pltpu.VMEM((2, 16, 8, 128), F32),
             pltpu.VMEM((n_row, 2, 32, 128), F32),
             [pltpu.VMEM(x.shape, x.dtype) for x in inputs],
             pltpu.VMEM((2, 8, 16, 128), F32),
             pltpu.VMEM((16, 16, 128), F32),
             pltpu.VMEM((2, 32, 512), F32),
             pltpu.VMEM((512, 128), F32),
-            pltpu.VMEM((2, 40, 128), F32),
+            pltpu.VMEM((2, 32, 128), F32),
+            pltpu.VMEM((2, 8, 128), F32),
             pltpu.VMEM((2, 32, 128), F32),
             pltpu.VMEM((32, 128), F32),
             pltpu.VMEM((8, 32, 128), F32),
@@ -405,14 +446,18 @@
             dma((16,)),
             dma((16,)),
             dma((16,)),
-            dma((n_row,)),
-            dma((n_row,)),
+            dma((16,)),
+            dma((16,)),
+            dma((4,)),
+            dma((4,)),
+            dma((4,)),
+            dma((4,)),
             dma((8,)),
             dma((8,)),
             dma((8,)),
             dma((8,)),
-            dma((5,)),
-            dma((5,)),
+            dma((6,)),
+            dma((6,)),
             dma((11,)),
             dma(()),
             pltpu.VMEM((2, 2, 512, 256), BF16),

time: 39.1 us -> 37.4 us (0.957)
  Pallas kernels: 38.4 us -> 36.7 us
    pallas_call x1, Pallas kernels: 36.2 us -> 34.4 us  [body(): pl.pallas_call(functools.partial(panel_kernel, n_row), out_shape=(jax.Sha...]
where the time goes in v3:
time: 37.4 us; the launch traced here: 37.3 us
  Pallas kernels  36.7 us (98%)
  between operations  0.64 us (2%)
    pallas_call x1, Pallas kernels, body(): pl.pallas_call(functools.partial(panel_kernel, n_row), out_shape=(jax.Sha...  34.4 us
    pallas_call x1, Pallas kernels, body(): pl.pallas_call(finish_kernel, out_shape=(jax.ShapeDtypeStruct((8192, 128)...  2.22 us

profile of v3, /device:TPU:1, one launch (start us, length us, event | category | flops | bytes accessed | tf_op | source)
XLA Modules:
  0.0 37.3 jit_solution(12981879944538973040)
XLA Ops:
  0.6 34.4 %panel.1 = (f32[8192,128]{1,0:T(8,128)S(1)}, f32[2,64,512]{2,1,0:T(8,128)S(1)}, f32[2,64,512]{2,1,0:T(8,128)S(1)}, f32[2,64,128]{2,1,0:T(8,128)S(1)}) custom-call(f32[8192,128]{1,0:T(8,128)} %bitcast.26, f32[2,32,512]{2,1,0:T(8,128)} %bitcast.27, f32[2,32,64]{2,1,0:T(8,128)} %bitcast.28, f32[2,32,64]{2,1,0:T(8,128)} %bitcast.29, f32[32,64]{1,0:T(8,128)} %bitcast.32, ...), custom_call_target="tpu_custom_call" | custom-call | tf_op jit(solution)/shard_map/panel/pallas_call | solution.py:416
  35.1 2.2 %finish.1 = (f32[8192,128]{1,0:T(8,128)}, f32[2,64,512]{2,1,0:T(8,128)}, f32[2,64,512]{2,1,0:T(8,128)}) custom-call(f32[8192,128]{1,0:T(8,128)S(1)} %get-tuple-element.10.trail, f32[2,64,512]{2,1,0:T(8,128)S(1)} %get-tuple-element.11.ranges, f32[2,64,512]{2,1,0:T(8,128)S(1)} %get-tuple-element.12.coeffs, f32[2,64,128]{2,1,0:T(8,128)S(1)} %get-tuple-element.13.inverses), custom_call_target="tpu_custom_call" | custom-call | tf_op jit(solution)/shard_map/finish/pallas_call | solution.py:471

commit v4 on v3

--- a/solution.py
+++ b/solution.py
@@ -137,20 +137,15 @@
     basis_full,
     chosen,
     updated,
-    pan_ss,
-    pan_rs,
-    xy_ss,
-    xy_rs,
-    pb_ss,
-    pb_rs,
-    zx_ss,
-    zx_rs,
-    zy_ss,
-    zy_rs,
-    rng_ss,
-    rng_rs,
-    c_ss,
-    c_rs,
+    pan_sems,
+    pb_sems,
+    xy_far,
+    xy_near,
+    xy_relay,
+    zx_sems,
+    zy_sems,
+    rng_sems,
+    c_sems,
     peer_ss,
     peer_rs,
     in_sem,
@@ -212,31 +207,39 @@
             device_id_type=MESH,
         )
 
-    sends = []
-
-    def send(*args):
-        one = copy(*args)
+    def send(src, dst, sems, row, col):
+        copy(src, dst, sems.at[0], sems.at[1], row, col).start()
+
+    def landed(ref, sems):
+        copy(ref, ref, sems.at[0], sems.at[1], r, peer).wait_recv()
+
+    def sent(ref, sems):
+        copy(ref, ref, sems.at[0], sems.at[1], r, peer).wait_send()
+
+    peer_copies = []
+
+    def to_peer(i, src, dst):
+        one = copy(src, dst, peer_ss.at[i], peer_rs.at[i], r, peer)
         one.start()
-        sends.append(one)
-
-    def to_peer(i, src, dst):
-        send(src, dst, peer_ss.at[i], peer_rs.at[i], r, peer)
+        peer_copies.append(one)
 
     def from_peer(i, ref):
         copy(ref, ref, peer_ss.at[i], peer_rs.at[i], r, peer).wait_recv()
 
     for d in order:
         to = (c + d) % 16
-        send(pan_send.at[to % 2, to // 2], pan_recv.at[c], pan_ss.at[d], pan_rs.at[c], r, to)
+        send(pan_send.at[to % 2, to // 2], pan_recv.at[c], pan_sems, r, to)
     for d in (2, 1, 3):
-        send(zg_send, zg.at[r], zx_ss.at[d], zx_rs.at[x], 4 * y + (x + d) % 4, c)
+        send(zg_send, zg.at[r], zx_sems, 4 * y + (x + d) % 4, c)
     for d in order:
         to = (c + d) % 16
-        send(pb_send.at[to % 2], pb.at[to % 2, c], pb_ss.at[d], pb_rs.at[c], r, to)
+        send(pb_send.at[to % 2], pb.at[to % 2, c], pb_sems, r, to)
     to_peer(0, panel.at[1 - k], pan_chip.at[k])
-    for d in order:
-        to = (c + d) % 16
-        send(xy_send.at[to % 2], xy.at[to % 2, c], xy_ss.at[d], xy_rs.at[c], r, to)
+    for d in (2, 6, 1, 7):
+        for core in range(2):
+            to = 2 * ((z + d) % 8) + core
+            send(xy_send.at[core], xy.at[core, c], xy_far if d in (2, 6) else xy_near, r, to)
+    send(xy_send.at[1 - k], xy.at[1 - k, c], xy_near, r, peer)
 
     trail_load.start()
     q_ids = lax.broadcasted_iota(jnp.int32, (512, 512), 0)
@@ -260,14 +263,10 @@
     scaled = select_dot(pair_apply(sketch[...]), chosen[...], NT)
 
     mine = pl.ds(pl.multiple_of(4 * y, 4), 4)
-    for d in range(1, 4):
-        at = (x + d) % 4
-        copy(zg.at[4 * y + at], zg.at[4 * y + at], zx_ss.at[0], zx_rs.at[at], 4 * y + at, c).wait_recv()
+    landed(zg.at[pl.ds(0, 3)], zx_sems)
     for d in (2, 1, 3):
-        send(zg.at[mine], zg.at[mine], zy_ss.at[d], zy_rs.at[y], 4 * ((y + d) % 4) + x, c)
-    for d in order:
-        at = (c + d) % 16
-        copy(pan_recv.at[at], pan_recv.at[at], pan_ss.at[0], pan_rs.at[at], r, at).wait_recv()
+        send(zg.at[mine], zg.at[mine], zy_sems, 4 * ((y + d) % 4) + x, c)
+    landed(pan_recv.at[pl.ds(0, 15)], pan_sems)
     for i in range(16):
         block = pan_recv[i]
         pan_full[32 * i : 32 * i + 16] = block
@@ -278,11 +277,16 @@
     steps = [4, 5, 3, 6, 2, 7, 1]
     for d in steps:
         to = 2 * ((z + d) % 8) + k
-        send(rng_send, rng_recv.at[z], rng_ss.at[d], rng_rs.at[z], r, to)
-
-    for d in order:
-        at = (c + d) % 16
-        copy(pb.at[k, at], pb.at[k, at], pb_ss.at[0], pb_rs.at[at], r, at).wait_recv()
+        send(rng_send, rng_recv.at[z], rng_sems, r, to)
+
+    landed(xy.at[0, pl.ds(0, 4)], xy_far)
+    for d, side in ((6, 1), (2, -1)):
+        origin = 2 * ((z + d) % 8)
+        both = xy.at[k, pl.ds(pl.multiple_of(origin, 2), 2)]
+        send(both, both, xy_relay, r, 2 * ((z + side) % 8) + k)
+        one = xy.at[k, origin + (d == 2)]
+        send(one, one, xy_relay, r, 2 * ((z + 2 * side) % 8) + k)
+    landed(pb.at[0, pl.ds(0, 15)], pb_sems)
     to_peer(5, pb.at[k], pb.at[k])
     from_peer(0, pan_chip.at[1 - k])
     from_peer(5, pb.at[1 - k])
@@ -295,9 +299,8 @@
     weights = dot(scaled, basis_full[...])[:, :64]
     mine = basis_full[pl.ds(pl.multiple_of(64 * z, 64), 64), :][:, :64]
     mixer = dot(jnp.concatenate([weights, mine], axis=0), pivot_scaled[...])
-    for d in order:
-        at = (c + d) % 16
-        copy(xy.at[k, at], xy.at[k, at], xy_ss.at[0], xy_rs.at[at], r, at).wait_recv()
+    landed(xy.at[0, pl.ds(0, 5)], xy_near)
+    landed(xy.at[0, pl.ds(0, 6)], xy_relay)
     to_peer(1, xy.at[k], xy.at[k])
     left = xy[k].reshape(512, 128)
     mixed = dot(mixer, left)
@@ -305,9 +308,7 @@
     fixes = dot(mixed, left, NT)
     updated[64:] = pan_chip[...].reshape(64, 512) - fixes[64:]
 
-    for d in steps:
-        at = (z + d) % 8
-        copy(rng_recv.at[at], rng_recv.at[at], rng_ss.at[0], rng_rs.at[at], r, 2 * at + k).wait_recv()
+    landed(rng_recv.at[pl.ds(0, 7)], rng_sems)
     total = unfold(rng_recv) - fixes[:64]
     updated[:64] = total
     ranges[k] = total
@@ -317,16 +318,16 @@
     c_recv[z] = folded
     for d in steps:
         to = 2 * ((z + d) % 8) + k
-        send(c_send, c_recv.at[z], c_ss.at[d], c_rs.at[z], r, to)
+        send(c_send, c_recv.at[z], c_sems, r, to)
     to_peer(2, ranges.at[k], ranges.at[k])
 
-    inverses[k] = swap(inverse_factor(products[:, :64] * (1.0 / 512.0)))
+    @pl.when(c < 16)
+    def _():
+        inverses[k] = swap(inverse_factor(products[:, :64] * (1.0 / 512.0)))
+
     to_peer(3, inverses.at[k], inverses.at[k])
     from_peer(1, xy.at[1 - k])
-    for d in range(1, 4):
-        at = (y + d) % 4
-        part = pl.ds(pl.multiple_of(4 * at, 4), 4)
-        copy(zg.at[part], zg.at[part], zy_ss.at[0], zy_rs.at[at], 4 * at + x, c).wait_recv()
+    landed(zg.at[pl.ds(0, 12)], zy_sems)
     trail_load.wait()
     low = lower_half((512, 128))
     columns = []
@@ -355,30 +356,37 @@
             lefts[a, b, :, :128] = high[:, 128 * b : 128 * b + 128]
             lefts[a, b, :, 128:] = rest[:, 128 * b : 128 * b + 128]
 
-    def change(a, part):
-        for b in range(2):
-            delta = bdot(lefts[a, b, 128 * part : 128 * part + 128], rights[b], NT)
-            for j in range(4):
-                lines = pl.ds(4096 * a + 1024 * part + 4 * b + j, 128, stride=8)
-                trail[lines, :] = trail[lines, :] - delta[:, 128 * j : 128 * j + 128]
-
-    for part in range(4):
-        change(0, part)
-
-    for d in steps:
-        at = (z + d) % 8
-        copy(c_recv.at[at], c_recv.at[at], c_ss.at[0], c_rs.at[at], r, 2 * at + k).wait_recv()
+    def change(a):
+        @pl.loop(0, 4)
+        def _(part):
+            for b in range(2):
+                delta = bdot(lefts[a, b, pl.ds(pl.multiple_of(128 * part, 128), 128)], rights[b], NT)
+                for j in range(4):
+                    lines = pl.ds(pl.multiple_of(4096 * a + 1024 * part, 1024) + 4 * b + j, 128, stride=8)
+                    trail[lines, :] = trail[lines, :] - delta[:, 128 * j : 128 * j + 128]
+
+    change(0)
+
+    landed(c_recv.at[pl.ds(0, 7)], c_sems)
     permuted = select_dot(unfold(c_recv), chosen[...], NN)
     coeffs[k] = pair_apply(permuted) * (512.0**-0.5)
     to_peer(4, coeffs.at[k], coeffs.at[k])
-    for part in range(4):
-        change(1, part)
+    change(1)
 
     from_peer(2, ranges.at[1 - k])
     from_peer(3, inverses.at[1 - k])
     from_peer(4, coeffs.at[1 - k])
-    for one in sends:
+    for one in peer_copies:
         one.wait_send()
+    sent(pan_recv.at[pl.ds(0, 15)], pan_sems)
+    sent(pb.at[0, pl.ds(0, 15)], pb_sems)
+    sent(xy.at[0, pl.ds(0, 4)], xy_far)
+    sent(xy.at[0, pl.ds(0, 5)], xy_near)
+    sent(xy.at[0, pl.ds(0, 6)], xy_relay)
+    sent(zg.at[pl.ds(0, 3)], zx_sems)
+    sent(zg.at[pl.ds(0, 12)], zy_sems)
+    sent(rng_recv.at[pl.ds(0, 7)], rng_sems)
+    sent(c_recv.at[pl.ds(0, 7)], c_sems)
 
 
 def finish_kernel(trail, ranges, coeffs, inverses, trail_out, basis_out, coeff_out, basis, coeff, sems):
@@ -442,20 +450,7 @@
             pltpu.VMEM((512, 128), F32),
             pltpu.VMEM((512, 512), BF16),
             pltpu.VMEM((128, 512), F32),
-            dma((16,)),
-            dma((16,)),
-            dma((16,)),
-            dma((16,)),
-            dma((16,)),
-            dma((16,)),
-            dma((4,)),
-            dma((4,)),
-            dma((4,)),
-            dma((4,)),
-            dma((8,)),
-            dma((8,)),
-            dma((8,)),
-            dma((8,)),
+            *[dma((2,))] * 9,
             dma((6,)),
             dma((6,)),
             dma((11,)),

time: 37.4 us -> 33.5 us (0.90)
  Pallas kernels: 36.7 us -> 32.7 us
    pallas_call x1, Pallas kernels: 34.4 us -> 30.5 us  [body(): pl.pallas_call(functools.partial(panel_kernel, n_row), out_shape=(jax.Sha...]
where the time goes in v4:
time: 33.5 us; the launch traced here: 33.4 us
  Pallas kernels  32.7 us (98%)
  between operations  0.64 us (2%)
    pallas_call x1, Pallas kernels, body(): pl.pallas_call(functools.partial(panel_kernel, n_row), out_shape=(jax.Sha...  30.5 us
    pallas_call x1, Pallas kernels, body(): pl.pallas_call(finish_kernel, out_shape=(jax.ShapeDtypeStruct((8192, 128)...  2.22 us

profile of v4, /device:TPU:1, one launch (start us, length us, event | category | flops | bytes accessed | tf_op | source)
XLA Modules:
  0.0 33.4 jit_solution(7262395484120971750)
XLA Ops:
  0.6 30.5 %panel.1 = (f32[8192,128]{1,0:T(8,128)S(1)}, f32[2,64,512]{2,1,0:T(8,128)S(1)}, f32[2,64,512]{2,1,0:T(8,128)S(1)}, f32[2,64,128]{2,1,0:T(8,128)S(1)}) custom-call(f32[8192,128]{1,0:T(8,128)} %bitcast.26, f32[2,32,512]{2,1,0:T(8,128)} %bitcast.27, f32[2,32,64]{2,1,0:T(8,128)} %bitcast.28, f32[2,32,64]{2,1,0:T(8,128)} %bitcast.29, f32[32,64]{1,0:T(8,128)} %bitcast.32, ...), custom_call_target="tpu_custom_call" | custom-call | tf_op jit(solution)/shard_map/panel/pallas_call | solution.py:424
  31.1 2.2 %finish.1 = (f32[8192,128]{1,0:T(8,128)}, f32[2,64,512]{2,1,0:T(8,128)}, f32[2,64,512]{2,1,0:T(8,128)}) custom-call(f32[8192,128]{1,0:T(8,128)S(1)} %get-tuple-element.10.trail, f32[2,64,512]{2,1,0:T(8,128)S(1)} %get-tuple-element.11.ranges, f32[2,64,512]{2,1,0:T(8,128)S(1)} %get-tuple-element.12.coeffs, f32[2,64,128]{2,1,0:T(8,128)S(1)} %get-tuple-element.13.inverses), custom_call_target="tpu_custom_call" | custom-call | tf_op jit(solution)/shard_map/finish/pallas_call | solution.py:466

commit v5 on v4

--- a/solution.py
+++ b/solution.py
@@ -65,6 +65,12 @@
         tops.append(jnp.where(low, even, swap(odd)))
         bottoms.append(jnp.where(low, swap(even), odd))
     return jnp.concatenate([jnp.concatenate(tops, axis=1), jnp.concatenate(bottoms, axis=1)], axis=0)
+
+
+def pair_apply(x, factors):
+    odd = lax.broadcasted_iota(jnp.int32, x.shape, 1) % 2 == 1
+    partner = jnp.where(odd, pltpu.roll(x, 1, 1), pltpu.roll(x, 511, 1))
+    return x * factors[0:1] + partner * factors[1:2]
 
 
 def inverse_factor(gram):
@@ -116,9 +122,11 @@
     trail_hbm,
     inputs,
     trail,
-    ranges,
-    coeffs,
+    bases,
     inverses,
+    crosses,
+    chosen,
+    factors,
     xy,
     pb,
     zg,
@@ -133,12 +141,13 @@
     rng_send,
     rng_recv,
     c_send,
-    c_recv,
     basis_full,
-    chosen,
-    updated,
+    panel_high,
+    panel_low,
+    ranges,
     pan_sems,
     pb_sems,
+    px_sems,
     xy_far,
     xy_near,
     xy_relay,
@@ -162,6 +171,8 @@
     y, x = r // 4, r % 4
     order = [8, 9, 7, 10, 6, 11, 5, 12, 4, 13, 3, 14, 2, 15, 1]
 
+    steps = [4, 5, 3, 6, 2, 7, 1]
+
     barrier = pltpu.get_barrier_semaphore()
     for d in order:
         pl.semaphore_signal(barrier, inc=1, device_id=(r, (c + d) % 16), device_id_type=MESH)
@@ -191,7 +202,7 @@
         zg_send[a, :, 64:] = col_scaled[a]
     pan_recv[c] = pan_send[k, z]
     xy[k, c] = xy_send[k]
-    pb[k, c] = pb_send[k]
+    pb[k, x % 2, z] = pb_send[x % 2]
     zg[r] = zg_send[...]
     pan_chip[k] = panel[k]
 
@@ -231,9 +242,8 @@
         send(pan_send.at[to % 2, to // 2], pan_recv.at[c], pan_sems, r, to)
     for d in (2, 1, 3):
         send(zg_send, zg.at[r], zx_sems, 4 * y + (x + d) % 4, c)
-    for d in order:
-        to = (c + d) % 16
-        send(pb_send.at[to % 2], pb.at[to % 2, c], pb_sems, r, to)
+    for d in steps:
+        send(pb_send.at[x % 2], pb.at[k, x % 2, z], pb_sems, r, 2 * ((z + d) % 8) + k)
     to_peer(0, panel.at[1 - k], pan_chip.at[k])
     for d in (2, 6, 1, 7):
         for core in range(2):
@@ -256,11 +266,8 @@
     alpha = jnp.where(twin, other / determinant, 1.0 / own)
     beta = jnp.where(twin, -offdiag / determinant, 0.0)
 
-    def pair_apply(x):
-        partner = jnp.where(odd, pltpu.roll(x, 1, 1), pltpu.roll(x, 511, 1))
-        return x * alpha + partner * beta
-
-    scaled = select_dot(pair_apply(sketch[...]), chosen[...], NT)
+    factors[...] = jnp.concatenate([alpha, beta, jnp.zeros((6, 512), F32)], axis=0)
+    scaled = select_dot(pair_apply(sketch[...], factors), chosen[...], NT)
 
     mine = pl.ds(pl.multiple_of(4 * y, 4), 4)
     landed(zg.at[pl.ds(0, 3)], zx_sems)
@@ -274,11 +281,12 @@
     folded = fold(dot(scaled, pan_full[...]))
     rng_send[...] = folded
     rng_recv[z] = folded
-    steps = [4, 5, 3, 6, 2, 7, 1]
     for d in steps:
         to = 2 * ((z + d) % 8) + k
         send(rng_send, rng_recv.at[z], rng_sems, r, to)
 
+    landed(pb.at[0, 0, pl.ds(0, 7)], pb_sems)
+    send(pb.at[k, x % 2], pb.at[k, x % 2], px_sems, 4 * y + x + 1 - 2 * (x % 2), c)
     landed(xy.at[0, pl.ds(0, 4)], xy_far)
     for d, side in ((6, 1), (2, -1)):
         origin = 2 * ((z + d) % 8)
@@ -286,45 +294,56 @@
         send(both, both, xy_relay, r, 2 * ((z + side) % 8) + k)
         one = xy.at[k, origin + (d == 2)]
         send(one, one, xy_relay, r, 2 * ((z + 2 * side) % 8) + k)
-    landed(pb.at[0, pl.ds(0, 15)], pb_sems)
+    landed(pb.at[0, 0], px_sems)
     to_peer(5, pb.at[k], pb.at[k])
     from_peer(0, pan_chip.at[1 - k])
     from_peer(5, pb.at[1 - k])
     for i in range(16):
         for half in range(2):
-            block = pb[half, i]
+            block = pb[i % 2, half, i // 2]
             at = 32 * i + 16 * half
             basis_full[at : at + 8] = block
             basis_full[at + 8 : at + 16] = swap(block)
     weights = dot(scaled, basis_full[...])[:, :64]
     mine = basis_full[pl.ds(pl.multiple_of(64 * z, 64), 64), :][:, :64]
     mixer = dot(jnp.concatenate([weights, mine], axis=0), pivot_scaled[...])
+    mixer_high, mixer_low = split2(mixer)
+    mixer_both = jnp.concatenate([mixer_high, mixer_low], axis=0)
     landed(xy.at[0, pl.ds(0, 5)], xy_near)
     landed(xy.at[0, pl.ds(0, 6)], xy_relay)
     to_peer(1, xy.at[k], xy.at[k])
-    left = xy[k].reshape(512, 128)
-    mixed = dot(mixer, left)
+    left_high, left_low = split2(xy[k].reshape(512, 128))
+    mixed = bdot(mixer_both, left_high)
+    mixed = (bdot(mixer_high, left_low) + mixed[128:]) + mixed[:128]
     mixed = jnp.where(lower_half((128, 128)), swap(mixed), 0.0)
-    fixes = dot(mixed, left, NT)
-    updated[64:] = pan_chip[...].reshape(64, 512) - fixes[64:]
+    mixed_high, mixed_low = split2(mixed)
+    fixes = bdot(mixed_high, left_low, NT) + bdot(
+        jnp.concatenate([mixed_high, mixed_low], axis=1), jnp.concatenate([left_high, left_high], axis=1), NT
+    )
+    panel_high[...], panel_low[...] = split2(pan_chip[...].reshape(64, 512) - fixes[64:])
 
     landed(rng_recv.at[pl.ds(0, 7)], rng_sems)
     total = unfold(rng_recv) - fixes[:64]
-    updated[:64] = total
-    ranges[k] = total
-    products = dot(total, updated[...], NT)
-    folded = fold(swap(products))
+    ranges[...] = total
+    total_high, total_low = split2(total)
+    cross = bdot(jnp.concatenate([total_high, total_low], axis=0), panel_high[...], NT)
+    cross = (bdot(total_high, panel_low[...], NT) + cross[64:]) + cross[:64]
+    cross = jnp.concatenate([cross, cross], axis=1)
+    folded = jnp.where(lower_half((32, 128)), cross[:32], cross[32:])
     c_send[...] = folded
-    c_recv[z] = folded
+    crosses[k, z] = folded
     for d in steps:
         to = 2 * ((z + d) % 8) + k
-        send(c_send, c_recv.at[z], c_sems, r, to)
-    to_peer(2, ranges.at[k], ranges.at[k])
+        send(c_send, crosses.at[k, z], c_sems, r, to)
 
     @pl.when(c < 16)
     def _():
-        inverses[k] = swap(inverse_factor(products[:, :64] * (1.0 / 512.0)))
-
+        total = ranges[...]
+        inverse = swap(inverse_factor(dot(total, total, NT) * (1.0 / 512.0)))
+        inverses[k] = inverse
+        bases[k] = dot(inverse[:, :64], total)
+
+    to_peer(2, bases.at[k], bases.at[k])
     to_peer(3, inverses.at[k], inverses.at[k])
     from_peer(1, xy.at[1 - k])
     landed(zg.at[pl.ds(0, 12)], zy_sems)
@@ -356,50 +375,49 @@
             lefts[a, b, :, :128] = high[:, 128 * b : 128 * b + 128]
             lefts[a, b, :, 128:] = rest[:, 128 * b : 128 * b + 128]
 
-    def change(a):
-        @pl.loop(0, 4)
-        def _(part):
-            for b in range(2):
-                delta = bdot(lefts[a, b, pl.ds(pl.multiple_of(128 * part, 128), 128)], rights[b], NT)
-                for j in range(4):
-                    lines = pl.ds(pl.multiple_of(4096 * a + 1024 * part, 1024) + 4 * b + j, 128, stride=8)
-                    trail[lines, :] = trail[lines, :] - delta[:, 128 * j : 128 * j + 128]
-
-    change(0)
-
-    landed(c_recv.at[pl.ds(0, 7)], c_sems)
-    permuted = select_dot(unfold(c_recv), chosen[...], NN)
-    coeffs[k] = pair_apply(permuted) * (512.0**-0.5)
-    to_peer(4, coeffs.at[k], coeffs.at[k])
-    change(1)
-
-    from_peer(2, ranges.at[1 - k])
+    def change(a, parts):
+        @pl.when(c < 16)
+        def _():
+            for part in parts:
+                for b in range(2):
+                    delta = bdot(lefts[a, b, 128 * part : 128 * part + 128], rights[b], NT)
+                    for j in range(4):
+                        lines = pl.ds(4096 * a + 1024 * part + 4 * b + j, 128, stride=8)
+                        trail[lines, :] = trail[lines, :] - delta[:, 128 * j : 128 * j + 128]
+
+    change(0, range(4))
+
+    landed(crosses.at[0, pl.ds(0, 7)], c_sems)
+    to_peer(4, crosses.at[k], crosses.at[k])
+    change(1, range(4))
+    from_peer(2, bases.at[1 - k])
     from_peer(3, inverses.at[1 - k])
-    from_peer(4, coeffs.at[1 - k])
+    from_peer(4, crosses.at[1 - k])
     for one in peer_copies:
         one.wait_send()
     sent(pan_recv.at[pl.ds(0, 15)], pan_sems)
-    sent(pb.at[0, pl.ds(0, 15)], pb_sems)
+    sent(pb.at[0, 0, pl.ds(0, 7)], pb_sems)
+    sent(pb.at[0, 0], px_sems)
     sent(xy.at[0, pl.ds(0, 4)], xy_far)
     sent(xy.at[0, pl.ds(0, 5)], xy_near)
     sent(xy.at[0, pl.ds(0, 6)], xy_relay)
     sent(zg.at[pl.ds(0, 3)], zx_sems)
     sent(zg.at[pl.ds(0, 12)], zy_sems)
     sent(rng_recv.at[pl.ds(0, 7)], rng_sems)
-    sent(c_recv.at[pl.ds(0, 7)], c_sems)
-
-
-def finish_kernel(trail, ranges, coeffs, inverses, trail_out, basis_out, coeff_out, basis, coeff, sems):
-    copies = [pltpu.make_async_copy(trail.at[pl.ds(2048 * i, 2048)], trail_out.at[pl.ds(2048 * i, 2048)], sems.at[i]) for i in range(4)]
+    sent(crosses.at[0, pl.ds(0, 7)], c_sems)
+
+
+def finish_kernel(trail, bases, inverses, crosses, chosen, factors, trail_out, basis_out, coeff_out, coeff, sems):
+    copies = [pltpu.make_async_copy(trail.at[pl.ds(1024 * i, 1024)], trail_out.at[pl.ds(1024 * i, 1024)], sems.at[i]) for i in range(8)]
+    copies.append(pltpu.make_async_copy(bases, basis_out, sems.at[8]))
     for one in copies:
         one.start()
+    both = jnp.concatenate([unfold(crosses.at[0]), unfold(crosses.at[1])], axis=0)
+    both = pair_apply(select_dot(both, chosen[...], NN), factors) * (512.0**-0.5)
     for a in range(2):
-        inverse = inverses[a][:, :64]
-        basis[a] = dot(inverse, ranges[a])
-        coeff[a] = dot(inverse, coeffs[a])
-    copies += [pltpu.make_async_copy(basis, basis_out, sems.at[4]), pltpu.make_async_copy(coeff, coeff_out, sems.at[5])]
-    for one in copies[4:]:
-        one.start()
+        coeff[a] = dot(inverses[a][:, :64], both[64 * a : 64 * a + 64])
+    copies.append(pltpu.make_async_copy(coeff, coeff_out, sems.at[9]))
+    copies[9].start()
     for one in copies:
         one.wait()
 
@@ -426,14 +444,16 @@
         out_shape=(
             jax.ShapeDtypeStruct((8192, 128), F32),
             small,
-            small,
             jax.ShapeDtypeStruct((2, 64, 128), F32),
+            jax.ShapeDtypeStruct((2, 8, 32, 128), F32),
+            jax.ShapeDtypeStruct((512, 512), BF16),
+            jax.ShapeDtypeStruct((8, 512), F32),
         ),
         in_specs=[HBM] * 12,
-        out_specs=(VMEM,) * 4,
+        out_specs=(VMEM,) * 6,
         scratch_shapes=[
             pltpu.VMEM((2, 16, 32, 128), F32),
-            pltpu.VMEM((2, 16, 8, 128), F32),
+            pltpu.VMEM((2, 2, 8, 8, 128), F32),
             pltpu.VMEM((n_row, 2, 32, 128), F32),
             [pltpu.VMEM(x.shape, x.dtype) for x in inputs],
             pltpu.VMEM((2, 8, 16, 128), F32),
@@ -446,11 +466,11 @@
             pltpu.VMEM((32, 128), F32),
             pltpu.VMEM((8, 32, 128), F32),
             pltpu.VMEM((32, 128), F32),
-            pltpu.VMEM((8, 32, 128), F32),
             pltpu.VMEM((512, 128), F32),
-            pltpu.VMEM((512, 512), BF16),
-            pltpu.VMEM((128, 512), F32),
-            *[dma((2,))] * 9,
+            pltpu.VMEM((64, 512), BF16),
+            pltpu.VMEM((64, 512), BF16),
+            pltpu.VMEM((64, 512), F32),
+            *[dma((2,))] * 10,
             dma((6,)),
             dma((6,)),
             dma((11,)),
@@ -466,9 +486,9 @@
     trail_out, basis_out, coeff_out = pl.pallas_call(
         finish_kernel,
         out_shape=(jax.ShapeDtypeStruct((8192, 128), F32), small, small),
-        in_specs=[VMEM] * 4,
+        in_specs=[VMEM] * 6,
         out_specs=(HBM,) * 3,
-        scratch_shapes=[pltpu.VMEM((2, 64, 512), F32), pltpu.VMEM((2, 64, 512), F32), dma((6,))],
+        scratch_shapes=[pltpu.VMEM((2, 64, 512), F32), dma((10,))],
         compiler_params=pltpu.CompilerParams(vmem_limit_bytes=40 * 1024 * 1024),
         name="finish",
     )(*results)

time: 33.5 us -> 32.4 us (0.967)
  Pallas kernels: 32.7 us -> 31.7 us
    pallas_call x1, Pallas kernels: 30.5 us -> 29.4 us  [body(): pl.pallas_call(functools.partial(panel_kernel, n_row), out_shape=(jax.Sha...]
where the time goes in v5:
time: 32.4 us; the launch traced here: 32.3 us
  Pallas kernels  31.7 us (98%)
  between operations  0.64 us (2%)
    pallas_call x1, Pallas kernels, body(): pl.pallas_call(functools.partial(panel_kernel, n_row), out_shape=(jax.Sha...  29.4 us
    pallas_call x1, Pallas kernels, body(): pl.pallas_call(finish_kernel, out_shape=(jax.ShapeDtypeStruct((8192, 128)...  2.25 us

profile of v5, /device:TPU:1, one launch (start us, length us, event | category | flops | bytes accessed | tf_op | source)
XLA Modules:
  0.0 32.3 jit_solution(14234897917981771069)
XLA Ops:
  0.6 29.4 %panel.1 = (f32[8192,128]{1,0:T(8,128)S(1)}, f32[2,64,512]{2,1,0:T(8,128)S(1)}, f32[2,64,128]{2,1,0:T(8,128)S(1)}, f32[2,8,32,128]{3,2,1,0:T(8,128)S(1)}, bf16[5...) custom-call(f32[8192,128]{1,0:T(8,128)} %bitcast.26, f32[2,32,512]{2,1,0:T(8,128)} %bitcast.27, f32[2,32,64]{2,1,0:T(8,128)} %bitcast.28, ...), custom_call_target="tpu_custom_call" | custom-call | tf_op jit(solution)/shard_map/panel/pallas_call | solution.py:442
  30.1 2.3 %finish.1 = (f32[8192,128]{1,0:T(8,128)}, f32[2,64,512]{2,1,0:T(8,128)}, f32[2,64,512]{2,1,0:T(8,128)}) custom-call(f32[8192,128]{1,0:T(8,128)S(1)} %get-tuple-element.12.trail, f32[2,64,512]{2,1,0:T(8,128)S(1)} %get-tuple-element.13.bases, f32[2,64,128]{2,1,0:T(8,128)S(1)} %get-tuple-element.14.inverses, f32[2,8,32,128]{3,2,1,0:T(8,128)S(1)} %get-tuple-element.15.crosses, ...), custom_call_target="tpu_custom_call" | custom-call | tf_op jit(solution)/shard_map/finish/pallas_call | solution.py:486

commit v6 on v5

--- a/solution.py
+++ b/solution.py
@@ -155,6 +155,7 @@
     zy_sems,
     rng_sems,
     c_sems,
+    hand_sems,
     peer_ss,
     peer_rs,
     in_sem,
@@ -331,10 +332,20 @@
     cross = jnp.concatenate([cross, cross], axis=1)
     folded = jnp.where(lower_half((32, 128)), cross[:32], cross[32:])
     c_send[...] = folded
-    crosses[k, z] = folded
+
+    def cross_copy(to):
+        return copy(c_send, crosses.at[k, z], c_sems.at[0], c_sems.at[1 + k], r, to)
+
     for d in steps:
-        to = 2 * ((z + d) % 8) + k
-        send(c_send, crosses.at[k, z], c_sems, r, to)
+        cross_copy(2 * ((z + d) % 8) + 1).start()
+
+    @pl.when(k == 0)
+    def _():
+        cross_copy(peer).start()
+
+    @pl.when(k == 1)
+    def _():
+        crosses[1, z] = folded
 
     @pl.when(c < 16)
     def _():
@@ -387,12 +398,25 @@
 
     change(0, range(4))
 
-    landed(crosses.at[0, pl.ds(0, 7)], c_sems)
-    to_peer(4, crosses.at[k], crosses.at[k])
+    def hand_over(a, count):
+        block = crosses.at[a, pl.ds(0, count)]
+        copy(block, block, c_sems.at[0], c_sems.at[1 + a], r, peer).wait_recv()
+        copy(crosses.at[a], crosses.at[a], hand_sems.at[a], hand_sems.at[2 + a], r, peer).start()
+
+    @pl.when(k == 1)
+    def _():
+        hand_over(1, 7)
+        hand_over(0, 8)
+
     change(1, range(4))
     from_peer(2, bases.at[1 - k])
     from_peer(3, inverses.at[1 - k])
-    from_peer(4, crosses.at[1 - k])
+
+    @pl.when(k == 0)
+    def _():
+        for a in (1, 0):
+            copy(crosses.at[a], crosses.at[a], hand_sems.at[a], hand_sems.at[2 + a], r, peer).wait_recv()
+
     for one in peer_copies:
         one.wait_send()
     sent(pan_recv.at[pl.ds(0, 15)], pan_sems)
@@ -404,20 +428,29 @@
     sent(zg.at[pl.ds(0, 3)], zx_sems)
     sent(zg.at[pl.ds(0, 12)], zy_sems)
     sent(rng_recv.at[pl.ds(0, 7)], rng_sems)
-    sent(crosses.at[0, pl.ds(0, 7)], c_sems)
+    copy(crosses.at[0, pl.ds(0, 7)], crosses.at[0, pl.ds(0, 7)], c_sems.at[0], c_sems.at[1], r, peer).wait_send()
+
+    @pl.when(k == 0)
+    def _():
+        cross_copy(peer).wait_send()
+
+    @pl.when(k == 1)
+    def _():
+        for a in (1, 0):
+            copy(crosses.at[a], crosses.at[a], hand_sems.at[a], hand_sems.at[2 + a], r, peer).wait_send()
 
 
 def finish_kernel(trail, bases, inverses, crosses, chosen, factors, trail_out, basis_out, coeff_out, coeff, sems):
-    copies = [pltpu.make_async_copy(trail.at[pl.ds(1024 * i, 1024)], trail_out.at[pl.ds(1024 * i, 1024)], sems.at[i]) for i in range(8)]
-    copies.append(pltpu.make_async_copy(bases, basis_out, sems.at[8]))
+    copies = [pltpu.make_async_copy(trail.at[pl.ds(2048 * i, 2048)], trail_out.at[pl.ds(2048 * i, 2048)], sems.at[i]) for i in range(4)]
+    copies.append(pltpu.make_async_copy(bases, basis_out, sems.at[4]))
     for one in copies:
         one.start()
     both = jnp.concatenate([unfold(crosses.at[0]), unfold(crosses.at[1])], axis=0)
     both = pair_apply(select_dot(both, chosen[...], NN), factors) * (512.0**-0.5)
     for a in range(2):
         coeff[a] = dot(inverses[a][:, :64], both[64 * a : 64 * a + 64])
-    copies.append(pltpu.make_async_copy(coeff, coeff_out, sems.at[9]))
-    copies[9].start()
+    copies.append(pltpu.make_async_copy(coeff, coeff_out, sems.at[5]))
+    copies[5].start()
     for one in copies:
         one.wait()
 
@@ -470,7 +503,9 @@
             pltpu.VMEM((64, 512), BF16),
             pltpu.VMEM((64, 512), BF16),
             pltpu.VMEM((64, 512), F32),
-            *[dma((2,))] * 10,
+            *[dma((2,))] * 9,
+            dma((3,)),
+            dma((4,)),
             dma((6,)),
             dma((6,)),
             dma((11,)),
@@ -488,7 +523,7 @@
         out_shape=(jax.ShapeDtypeStruct((8192, 128), F32), small, small),
         in_specs=[VMEM] * 6,
         out_specs=(HBM,) * 3,
-        scratch_shapes=[pltpu.VMEM((2, 64, 512), F32), dma((10,))],
+        scratch_shapes=[pltpu.VMEM((2, 64, 512), F32), dma((6,))],
         compiler_params=pltpu.CompilerParams(vmem_limit_bytes=40 * 1024 * 1024),
         name="finish",
     )(*results)

time: 32.4 us -> 31.9 us (0.985)
  Pallas kernels: 31.7 us -> 31.1 us
    pallas_call x1, Pallas kernels: 29.4 us -> 28.9 us  [body(): pl.pallas_call(functools.partial(panel_kernel, n_row), out_shape=(jax.Sha...]
where the time goes in v6:
time: 31.9 us; the launch traced here: 31.8 us
  Pallas kernels  31.1 us (97%)
  between operations  0.64 us (2%)
    pallas_call x1, Pallas kernels, body(): pl.pallas_call(functools.partial(panel_kernel, n_row), out_shape=(jax.Sha...  28.9 us
    pallas_call x1, Pallas kernels, body(): pl.pallas_call(finish_kernel, out_shape=(jax.ShapeDtypeStruct((8192, 128)...  2.22 us

profile of v6, /device:TPU:1, one launch (start us, length us, event | category | flops | bytes accessed | tf_op | source)
XLA Modules:
  0.0 31.8 jit_solution(11756168127856573024)
XLA Ops:
  0.6 28.9 %panel.1 = (f32[8192,128]{1,0:T(8,128)S(1)}, f32[2,64,512]{2,1,0:T(8,128)S(1)}, f32[2,64,128]{2,1,0:T(8,128)S(1)}, f32[2,8,32,128]{3,2,1,0:T(8,128)S(1)}, bf16[5...) custom-call(f32[8192,128]{1,0:T(8,128)} %bitcast.26, f32[2,32,512]{2,1,0:T(8,128)} %bitcast.27, f32[2,32,64]{2,1,0:T(8,128)} %bitcast.28, ...), custom_call_target="tpu_custom_call" | custom-call | tf_op jit(solution)/shard_map/panel/pallas_call | solution.py:475
  29.6 2.2 %finish.1 = (f32[8192,128]{1,0:T(8,128)}, f32[2,64,512]{2,1,0:T(8,128)}, f32[2,64,512]{2,1,0:T(8,128)}) custom-call(f32[8192,128]{1,0:T(8,128)S(1)} %get-tuple-element.12.trail, f32[2,64,512]{2,1,0:T(8,128)S(1)} %get-tuple-element.13.bases, f32[2,64,128]{2,1,0:T(8,128)S(1)} %get-tuple-element.14.inverses, f32[2,8,32,128]{3,2,1,0:T(8,128)S(1)} %get-tuple-element.15.crosses, ...), custom_call_target="tpu_custom_call" | custom-call | tf_op jit(solution)/shard_map/finish/pallas_call | solution.py:521

commit v7 on v6

--- a/solution.py
+++ b/solution.py
@@ -156,7 +156,7 @@
     rng_sems,
     c_sems,
     hand_sems,
-    peer_ss,
+    out_sem,
     peer_rs,
     in_sem,
     trail_sem,
@@ -220,23 +220,16 @@
         )
 
     def send(src, dst, sems, row, col):
-        copy(src, dst, sems.at[0], sems.at[1], row, col).start()
+        copy(src, dst, out_sem, sems.at[0], row, col).start()
 
     def landed(ref, sems):
-        copy(ref, ref, sems.at[0], sems.at[1], r, peer).wait_recv()
-
-    def sent(ref, sems):
-        copy(ref, ref, sems.at[0], sems.at[1], r, peer).wait_send()
-
-    peer_copies = []
+        copy(ref, ref, out_sem, sems.at[0], r, peer).wait_recv()
 
     def to_peer(i, src, dst):
-        one = copy(src, dst, peer_ss.at[i], peer_rs.at[i], r, peer)
-        one.start()
-        peer_copies.append(one)
+        copy(src, dst, out_sem, peer_rs.at[i], r, peer).start()
 
     def from_peer(i, ref):
-        copy(ref, ref, peer_ss.at[i], peer_rs.at[i], r, peer).wait_recv()
+        copy(ref, ref, out_sem, peer_rs.at[i], r, peer).wait_recv()
 
     for d in order:
         to = (c + d) % 16
@@ -417,17 +410,8 @@
         for a in (1, 0):
             copy(crosses.at[a], crosses.at[a], hand_sems.at[a], hand_sems.at[2 + a], r, peer).wait_recv()
 
-    for one in peer_copies:
-        one.wait_send()
-    sent(pan_recv.at[pl.ds(0, 15)], pan_sems)
-    sent(pb.at[0, 0, pl.ds(0, 7)], pb_sems)
-    sent(pb.at[0, 0], px_sems)
-    sent(xy.at[0, pl.ds(0, 4)], xy_far)
-    sent(xy.at[0, pl.ds(0, 5)], xy_near)
-    sent(xy.at[0, pl.ds(0, 6)], xy_relay)
-    sent(zg.at[pl.ds(0, 3)], zx_sems)
-    sent(zg.at[pl.ds(0, 12)], zy_sems)
-    sent(rng_recv.at[pl.ds(0, 7)], rng_sems)
+    all_sent = trail.at[pl.ds(0, 2 * 1556)]
+    copy(all_sent, all_sent, out_sem, c_sems.at[1], r, peer).wait_send()
     copy(crosses.at[0, pl.ds(0, 7)], crosses.at[0, pl.ds(0, 7)], c_sems.at[0], c_sems.at[1], r, peer).wait_send()
 
     @pl.when(k == 0)
@@ -503,10 +487,10 @@
             pltpu.VMEM((64, 512), BF16),
             pltpu.VMEM((64, 512), BF16),
             pltpu.VMEM((64, 512), F32),
-            *[dma((2,))] * 9,
+            *[dma((1,))] * 9,
             dma((3,)),
             dma((4,)),
-            dma((6,)),
+            dma(()),
             dma((6,)),
             dma((11,)),
             dma(()),

time: 31.9 us -> 31.8 us (level)
  no operation moved by 1% of the time
where the time goes in v7:
time: 31.8 us; the launch traced here: 31.7 us
  Pallas kernels  31 us (97%)
  between operations  0.64 us (2%)
    pallas_call x1, Pallas kernels, body(): pl.pallas_call(functools.partial(panel_kernel, n_row), out_shape=(jax.Sha...  28.8 us
    pallas_call x1, Pallas kernels, body(): pl.pallas_call(finish_kernel, out_shape=(jax.ShapeDtypeStruct((8192, 128)...  2.22 us

profile of v7, /device:TPU:1, one launch (start us, length us, event | category | flops | bytes accessed | tf_op | source)
XLA Modules:
  0.0 31.7 jit_solution(17746192351425954859)
XLA Ops:
  0.6 28.8 %panel.1 = (f32[8192,128]{1,0:T(8,128)S(1)}, f32[2,64,512]{2,1,0:T(8,128)S(1)}, f32[2,64,128]{2,1,0:T(8,128)S(1)}, f32[2,8,32,128]{3,2,1,0:T(8,128)S(1)}, bf16[5...) custom-call(f32[8192,128]{1,0:T(8,128)} %bitcast.26, f32[2,32,512]{2,1,0:T(8,128)} %bitcast.27, f32[2,32,64]{2,1,0:T(8,128)} %bitcast.28, ...), custom_call_target="tpu_custom_call" | custom-call | tf_op jit(solution)/shard_map/panel/pallas_call | solution.py:459
  29.4 2.2 %finish.1 = (f32[8192,128]{1,0:T(8,128)}, f32[2,64,512]{2,1,0:T(8,128)}, f32[2,64,512]{2,1,0:T(8,128)}) custom-call(f32[8192,128]{1,0:T(8,128)S(1)} %get-tuple-element.12.trail, f32[2,64,512]{2,1,0:T(8,128)S(1)} %get-tuple-element.13.bases, f32[2,64,128]{2,1,0:T(8,128)S(1)} %get-tuple-element.14.inverses, f32[2,8,32,128]{3,2,1,0:T(8,128)S(1)} %get-tuple-element.15.crosses, ...), custom_call_target="tpu_custom_call" | custom-call | tf_op jit(solution)/shard_map/finish/pallas_call | solution.py:505
